TPU v7x, 256 devices: a whole 4x4x8 slice. The times are simulated.
256 devices in a mesh: dp: 16 (over z_lo, x, core), tensor: 16 (over z_hi, y).
Axes of the slice: x: 4, y: 4, z: 8 (z_hi: 4, z_lo: 2; z = z_hi * 2 + z_lo), core: 2. Of those that a mesh axis runs over, the one named last changes fastest.
Arguments:
- activations: bfloat16 [4096, 5120], P('dp'), may hold values from -6 to 6
- grad_out: bfloat16 [4096, 5120], P('dp'), may hold values from -6 to 6
- gate_pre: bfloat16 [4096, 7168], P('dp', 'tensor'), may hold values from -8 to 8
- up_pre: bfloat16 [4096, 7168], P('dp', 'tensor'), may hold values from -6 to 6
- gate_up: bfloat16 [5120, 2, 7168], P('dp', None, 'tensor'), may hold values from -0.078125 to 0.078125
- down_weight: bfloat16 [5120, 7168], P('dp', 'tensor'), may hold values from -0.0625 to 0.0625
Outputs:
- grad_input: bfloat16 [4096, 5120], P('dp')
- grad_gate_up: float32 [5120, 2, 7168], P('dp', None, 'tensor')
- grad_down: float32 [5120, 7168], P('dp', 'tensor')
All inputs are finite; a program needn't handle non-finite values.
Results may differ from a plain program's by a relative error of at most 0.017.
Values may be sent and summed in bfloat16 or wider, within the bound.
A program may use at most 128 MiB of HBM per device.

v0:
```python
import jax
import jax.numpy as jnp
from jax import lax
from jax.sharding import Mesh
from jax.sharding import PartitionSpec as P

DP = ("dp_0", "dp_1", "dp_2")
TENSOR = ("tensor_0", "tensor_1")


def sum_in_order(pieces, axes, order):
    dims = [lax.axis_size(a) for a in axes]
    pieces = pieces.reshape(*dims, *pieces.shape[1:])
    pieces = pieces.transpose(*order, *range(len(axes), pieces.ndim))
    pieces = pieces.reshape(-1, *pieces.shape[len(axes) :])
    for k in order:
        pieces = lax.psum_scatter(pieces, axes[k], scatter_dimension=0, tiled=True)
    return pieces[0]


def split_up(x, dim, devices):
    dims = x.shape
    pieces = x.reshape(*dims[:dim], devices, dims[dim] // devices, *dims[dim + 1 :])
    return jnp.moveaxis(pieces, dim, 0)


def sum_by_axis(x, axes, order, dim):
    devices = lax.axis_size(axes)
    return sum_in_order(split_up(x, dim, devices), axes, order)


def sum_at_owner(x, axis, dim):
    devices = lax.axis_size(axis)
    pieces = lax.all_to_all(split_up(x, dim, devices), axis, 0, 0, tiled=True)
    return jnp.sum(pieces.astype(jnp.float32), axis=0)


def sum_in_two_steps(x, axes, dim):
    far, near = axes
    own = sum_at_owner(split_up(x, dim, lax.axis_size(far)), near, dim + 1)
    return jnp.sum(
        lax.all_to_all(own.astype(jnp.bfloat16), far, 0, 0, tiled=True).astype(jnp.float32), axis=0
    )


def per_device(activations, grad_out, gate_pre, up_pre, gate_up, down_weight):
    tokens = activations.shape[0]
    hidden_width = down_weight.shape[1]
    dp_count = lax.axis_size(DP)
    slab_rows = down_weight.shape[0]
    gate_wide = gate_pre.astype(jnp.float32)
    up_wide = up_pre.astype(jnp.float32)
    gate_sigmoid = jax.nn.sigmoid(gate_wide)
    gate_silu = gate_wide * gate_sigmoid
    hidden = (gate_silu * up_wide).astype(jnp.bfloat16)
    grad_h = jnp.dot(
        grad_out,
        lax.all_gather(down_weight, DP, axis=0, tiled=True),
        preferred_element_type=jnp.float32,
    )
    grad_gate = grad_h * up_wide * gate_sigmoid * (1.0 + gate_wide * (1.0 - gate_sigmoid))
    grad_up = grad_h * gate_silu
    grad_hidden = (
        jnp.stack([grad_gate, grad_up], axis=1)
        .astype(jnp.bfloat16)
        .reshape(tokens, 2 * hidden_width)
    )
    pieces = lax.all_gather(gate_up, DP, axis=0, tiled=True)
    flattened = pieces.reshape(pieces.shape[0], 2 * hidden_width)
    partial_sum = lax.dot_general(
        grad_hidden, flattened, (((1,), (1,)), ((), ())), preferred_element_type=jnp.float32
    )
    share_block = sum_by_axis(partial_sum.astype(jnp.bfloat16), TENSOR, (1, 0), 0).astype(
        jnp.float32
    )
    grad_input = lax.all_gather(share_block.astype(jnp.bfloat16), TENSOR, axis=0, tiled=True)
    gate_part = lax.dot_general(
        activations, grad_hidden, (((0,), (0,)), ((), ())), preferred_element_type=jnp.float32
    )
    down_part = lax.dot_general(
        grad_out, hidden, (((0,), (0,)), ((), ())), preferred_element_type=jnp.float32
    )
    summed = sum_in_two_steps(
        jnp.concatenate([gate_part, down_part], axis=1).astype(jnp.bfloat16),
        (("dp_0", "dp_1"), "dp_2"),
        0,
    )
    summed = summed / dp_count
    grad_gate_up = summed[:, : 2 * hidden_width].reshape(slab_rows, 2, hidden_width)
    grad_down = summed[:, 2 * hidden_width :]
    return (grad_input, grad_gate_up, grad_down)


def solution(mesh):
    split = Mesh(
        mesh.devices.reshape(2, 4, 2, 4, 4), ("dp_0", "dp_1", "dp_2", "tensor_0", "tensor_1")
    )
    return jax.shard_map(
        per_device,
        mesh=split,
        in_specs=(
            P(DP, None),
            P(DP, None),
            P(DP, TENSOR),
            P(DP, TENSOR),
            P(DP, None, TENSOR),
            P(DP, TENSOR),
        ),
        out_specs=(P(DP, None), P(DP, None, TENSOR), P(DP, TENSOR)),
        check_vma=False,
    )
```

profile of v0, /device:TPU:8, one launch (start us, length us, event | category | flops | bytes accessed | tf_op | source)
XLA Modules:
  0.0 286.2 jit_solution(15581350529174634229)
XLA Ops:
  7.2 0.7 all-gather.5.cloned.1.call-update
  8.0 2.0 copy.20
  10.0 5.5 %fusion = bf16[5120,448]{0,1:T(8,128)(2,1)} fusion(bf16[256,5120]{1,0:T(8,128)(2,1)} %param.7, bf16[256,448]{0,1:T(8,128)(2,1)} %param.9, bf16[256,448]{0,1:T(8,128)(2,1)} %param.8), kind=kOutput, calls=%fused_computation.5 | convolution fusion | flops 1177616384 | bytes 7667712 | tf_op jit(solution)/shard_map/dot_general | solution.py:80
  15.5 7.7 %copy.23 = bf16[5120,448]{1,0:T(8,128)(2,1)} copy(bf16[5120,448]{0,1:T(8,128)(2,1)} %fusion) | data formatting | bytes 9175040 | tf_op jit(solution)/shard_map/dot_general | solution.py:80
  23.1 31.5 %all-gather.5.cloned.1.call-done = bf16[5120,448]{1,0:T(8,128)(2,1)} async-done(((bf16[320,448]{1,0:T(8,128)(2,1)}), bf16[5120,448]{1,0:T(8,128)(2,1)}) %all-gather.5.cloned.1.call-update) | async-done | bytes 4587536 | tf_op jit(solution)/shard_map/all_gather | solution.py:58
  54.6 5.4 %fusion.4 = (bf16[256,1,448]{0,2,1:T(8,128)(2,1)S(1)}, bf16[256,1,448]{0,2,1:T(8,128)(2,1)S(1)}) fusion(bf16[256,448]{0,1:T(8,128)(2,1)S(1)} %copy-done.2, bf16[256,448]{0,1:T(8,128)(2,1)S(1)} %copy-done.3, bf16[256,5120]{1,0:T(8,128)(2,1)} %param.7, bf16[5120,448]{1,0:T(8,128)(2,1)} %all-gather.5.cloned.1.call-done), kind=kOutput, calls=%fused_computation.16 | convolution fusion | flops 1176125440 | bytes 8126464 | tf_op jit(solution)/shard_map/dot_general | solution.py:56
  60.0 6.0 %convert_bitcast_fusion = bf16[5120,896]{0,1:T(8,128)(2,1)} fusion(bf16[256,896]{0,1:T(8,128)(2,1)S(1)} %bitcast.33, bf16[256,5120]{1,0:T(8,128)(2,1)S(1)} %copy-done), kind=kOutput, calls=%fused_computation.2 | convolution fusion | flops 2353397760 | bytes 12255232 | tf_op jit(solution)/shard_map/dot_general | solution.py:77
  66.1 12.9 %copy.22 = bf16[5120,896]{1,0:T(8,128)(2,1)} copy(bf16[5120,896]{0,1:T(8,128)(2,1)} %convert_bitcast_fusion) | data formatting | bytes 18350080 | tf_op jit(solution)/shard_map/dot_general | solution.py:77
  79.0 7.7 %maximum_bitcast_fusion = bf16[2,8,320,1344]{3,2,0,1:T(8,128)(2,1)S(1)} fusion(bf16[8,2,320,448]{3,2,1,0:T(8,128)(2,1)} %bitcast.29, bf16[8,2,320,896]{3,2,1,0:T(8,128)(2,1)} %bitcast.28), kind=kLoop, calls=%fused_computation | loop fusion | flops 27525120 | bytes 27525120 | tf_op jit(solution)/shard_map/transpose | solution.py:24
  86.7 3.6 %copy.24 = bf16[2,8,320,1344]{3,2,1,0:T(8,128)(2,1)S(1)} copy(bf16[2,8,320,1344]{3,2,0,1:T(8,128)(2,1)S(1)} %maximum_bitcast_fusion) | data formatting | bytes 27525120 | tf_op jit(solution)/shard_map/transpose | solution.py:24
  90.4 18.7 %all_to_all.10 = bf16[2,8,320,1344]{3,2,1,0:T(8,128)(2,1)} all-to-all(bf16[2,8,320,1344]{3,2,1,0:T(8,128)(2,1)S(1)} %copy.24), channel_id=1, replica_groups=mesh['dp_0'=2,'dp_1'=4,'dp_2'=2,'tensor_0'=4,'tensor_1'=4] {'dp_2'}, dimensions={0} | all-to-all | bytes 27525120 | tf_op jit(solution)/shard_map/all_to_all | solution.py:34
  109.1 13.1 %reduce_sum.21 = bf16[8,320,1344]{2,1,0:T(8,128)(2,1)} reduce(bf16[2,8,320,1344]{3,2,1,0:T(8,128)(2,1)} %all_to_all.10, bf16[]{:T(256)} %constant.6.clone.1), dimensions={0}, to_apply=%region_2.0 | reduce | flops 3440640 | bytes 20643842 | tf_op jit(solution)/shard_map/reduce_sum | solution.py:35
  122.1 4.8 %all-to-all-start.1 = ((bf16[8,320,1344]{2,1,0:T(8,128)(2,1)}), bf16[8,320,1344]{2,1,0:T(8,128)(2,1)}, u32[]{:S(2)}, u32[]{:S(2)}) async-start(bf16[8,320,1344]{2,1,0:T(8,128)(2,1)} %reduce_sum.21), calls=%async_computation.3 | async-start | bytes 14417920 | tf_op jit(solution)/shard_map/all_to_all | solution.py:42
  127.2 11.1 %fusion.1 = bf16[256,5120]{1,0:T(8,128)(2,1)S(1)} fusion(bf16[5120,2,448]{2,0,1:T(8,128)(2,1)} %all-gather.7.cloned.1.call-done, bf16[256,1,448]{0,2,1:T(8,128)(2,1)S(1)} %get-tuple-element.4, bf16[256,1,448]{0,2,1:T(8,128)(2,1)S(1)} %get-tuple-element.3), kind=kOutput, calls=%fused_computation.6 | convolution fusion | flops 2350350336 | bytes 12255232 | tf_op jit(solution)/shard_map/dot_general | solution.py:70
  138.3 1.7 copy.21
  140.1 36.3 %reduce-scatter.3.cloned.1.call-done = bf16[4,16,5120]{2,1,0:T(8,128)(2,1)} async-done(((bf16[16,16,5120]{2,1,0:T(8,128)(2,1)}), bf16[4,16,5120]{2,1,0:T(8,128)(2,1)}) %reduce-scatter.3.cloned.1.call-update) | async-done | bytes 655376 | tf_op jit(solution)/shard_map/reduce_scatter | solution.py:17
  176.5 36.1 %reduce-scatter.5.cloned.1.call-done = bf16[1,16,5120]{2,1,0:T(8,128)(2,1)} async-done(((bf16[4,16,5120]{2,1,0:T(8,128)(2,1)}), bf16[1,16,5120]{2,1,0:T(8,128)(2,1)}) %reduce-scatter.5.cloned.1.call-update) | async-done | bytes 163856 | tf_op jit(solution)/shard_map/reduce_scatter | solution.py:17
  212.6 5.2 %all-to-all-done.1 = bf16[8,320,1344]{2,1,0:T(8,128)(2,1)} async-done(((bf16[8,320,1344]{2,1,0:T(8,128)(2,1)}), bf16[8,320,1344]{2,1,0:T(8,128)(2,1)}, u32[]{:S(2)}, u32[]{:S(2)}) %all-to-all-start.1) | async-done | bytes 6881312 | tf_op jit(solution)/shard_map/all_to_all | solution.py:42
  217.8 4.3 %convert_reduce_fusion = f32[320,1344]{1,0:T(8,128)S(1)} fusion(bf16[8,320,1344]{2,1,0:T(8,128)(2,1)} %all-to-all-done.1), kind=kLoop, calls=%fused_computation.1 | loop fusion | flops 6451200 | bytes 8601600 | tf_op jit(solution)/shard_map/reduce_sum | solution.py:41
  222.2 1.1 slice.8
  223.3 0.9 slice.9
  224.2 3.5 %reshape.21 = f32[320,2,448]{2,1,0:T(2,128)} reshape(f32[320,896]{1,0:T(8,128)} %slice.8) | data formatting | bytes 2293760 | tf_op jit(solution)/shard_map/reshape | solution.py:89
  227.8 48.5 %all-gather.9.cloned.1.call-done = bf16[1,256,5120]{2,1,0:T(8,128)(2,1)} async-done(((bf16[1,16,5120]{2,1,0:T(8,128)(2,1)}), bf16[1,256,5120]{2,1,0:T(8,128)(2,1)}) %all-gather.9.cloned.1.call-update) | async-done | bytes 2621456 | tf_op jit(solution)/shard_map/all_gather | solution.py:76
  276.3 3.4 %copy.26 = bf16[256,5120]{1,0:T(8,128)(2,1)} copy(bf16[256,5120]{1,0:T(8,128)(2,1)} %bitcast.31) | data formatting | bytes 5242880
  (20 shorter events, 0.7 us)
Async XLA Ops:
  7.2 52.9 %copy-start = (bf16[256,5120]{1,0:T(8,128)(2,1)S(1)}, bf16[256,5120]{1,0:T(8,128)(2,1)}, u32[]{:S(2)}) copy-start(bf16[256,5120]{1,0:T(8,128)(2,1)} %param.6) | copy-start | bytes 7864324
  7.2 47.4 %all-gather.5.cloned.1.call-start = ((), (), s32[]{:S(2)}) async-start(), calls=%async_computation.4 | async-start | bytes 5570560 | tf_op jit(solution)/shard_map/all_gather | solution.py:58
  7.9 119.3 %all-gather.7.cloned.1.call-start = ((), (), s32[]{:S(2)}) async-start(), calls=%async_computation.5 | async-start | bytes 11141120 | tf_op jit(solution)/shard_map/all_gather | solution.py:68
  15.5 39.1 %copy-start.2 = (bf16[256,448]{0,1:T(8,128)(2,1)S(1)}, bf16[256,448]{0,1:T(8,128)(2,1)}, u32[]{:S(2)}) copy-start(bf16[256,448]{0,1:T(8,128)(2,1)} %param.9) | copy-start | bytes 688132
  15.5 39.1 %copy-start.3 = (bf16[256,448]{0,1:T(8,128)(2,1)S(1)}, bf16[256,448]{0,1:T(8,128)(2,1)}, u32[]{:S(2)}) copy-start(bf16[256,448]{0,1:T(8,128)(2,1)} %param.8) | copy-start | bytes 688132
  122.1 95.7 %all-to-all-start.1 = ((bf16[8,320,1344]{2,1,0:T(8,128)(2,1)}), bf16[8,320,1344]{2,1,0:T(8,128)(2,1)}, u32[]{:S(2)}, u32[]{:S(2)}) async-start(bf16[8,320,1344]{2,1,0:T(8,128)(2,1)} %reduce_sum.21), calls=%async_computation.3 | async-start | bytes 14417920 | tf_op jit(solution)/shard_map/all_to_all | solution.py:42
  127.0 49.4 %reduce-scatter.3.cloned.1.call-start = ((), (), s32[]{:S(2)}) async-start(), calls=%async_computation.6 | async-start | bytes 3276800 | tf_op jit(solution)/shard_map/reduce_scatter | solution.py:17
  140.1 72.5 %reduce-scatter.5.cloned.1.call-start = ((), (), s32[]{:S(2)}) async-start(), calls=%async_computation.7 | async-start | bytes 819200 | tf_op jit(solution)/shard_map/reduce_scatter | solution.py:17
  176.4 99.8 %all-gather.9.cloned.1.call-start = ((), (), s32[]{:S(2)}) async-start(), calls=%async_computation.8 | async-start | bytes 2785280 | tf_op jit(solution)/shard_map/all_gather | solution.py:76
  222.1 57.6 %copy-start.1 = (bf16[256,5120]{1,0:T(8,128)(2,1)S(1)}, bf16[256,5120]{1,0:T(8,128)(2,1)}, u32[]{:S(2)}) copy-start(bf16[256,5120]{1,0:T(8,128)(2,1)} %param.6) | copy-start | bytes 7864324
Sparse Core Ops, SparseCore 0:
  9.8 44.6 all-gather.4
  56.9 64.1 all-gather.6
  140.2 36.1 reduce-scatter.2
  178.8 33.7 reduce-scatter.4
  214.9 61.3 all-gather.8
where the time goes:
time: 288 us; the launch traced here: 286 us
  waiting for transfers between devices  158 us (55%)
  local copies, waits for them, and re-layouts  36.9 us (13%)
  matrix products  28 us (10%)
  other arithmetic  25.3 us (9%)
  blocking collectives  18.7 us (6%)
  between operations  13.9 us (5%)
  starting transfers between devices  5.22 us (2%)
    reduce_scatter x2, waiting for transfers between devices, sum_in_order(): pieces = lax.psum_scatter(pieces, axes[k], scatter_dimension=0, tiled=True)  72.4 us
    all_gather x1, waiting for transfers between devices, per_device(): lax.all_gather(share_block.astype(jnp.bfloat16), TENSOR, axis=0, tiled=True)  48.5 us
    all_gather x1, waiting for transfers between devices, per_device(): lax.all_gather(down_weight, DP, axis=0, tiled=True)  31.5 us
    all_to_all x1, blocking collectives, sum_at_owner(): pieces = lax.all_to_all(split_up(x, dim, devices), axis, 0, 0, tiled=True)  18.7 us
    reduce_sum x1, other arithmetic, sum_at_owner(): return jnp.sum(pieces.astype(jnp.float32), axis=0)  13.1 us
    dot_general x1, local copies, waits for them, and re-layouts, per_device(): lax.dot_general(activations, grad_hidden, (((0,), (0,)), ((), ())), prefe...  12.9 us
    dot_general x1, matrix products, per_device(): lax.dot_general(grad_hidden, flattened, (((1,), (1,)), ((), ())), preferr...  11.1 us
    transpose x1, other arithmetic, split_up(): return jnp.moveaxis(pieces, dim, 0)  7.72 us
  transfers between devices with their start and end apart: 6, of which 5 were waited for; matrix products, arithmetic and copies ran while one was open for 30% of the time, Pallas kernels for 0%

commit v1 on v0

v1 whole, which is shorter than its diff:
```python
import jax
import jax.numpy as jnp
from jax import lax
from jax.experimental import pallas as pl
from jax.experimental.pallas import tpu as pltpu
from jax.sharding import Mesh
from jax.sharding import PartitionSpec as P

Z, X, C, H, Y = "dp_0", "dp_1", "dp_2", "tensor_0", "tensor_1"
DP = (Z, X, C)
TENSOR = (H, Y)
BF = jnp.bfloat16
F32 = jnp.float32

TOK = 256
D = 5120
DH = D // 2
SLAB = 640
ROWS = 320
HALF = 160
FD = 448
FG = 896
QT = 64
HT = 16


class Sems:
    def __init__(self):
        self.n = 0

    def block(self, count=1):
        first = self.n
        self.n += count
        return first


def wgrad_slab(acts, right, xs):
    cols = pl.ds(pl.multiple_of(xs * SLAB, 128), SLAB)
    return lax.dot_general(
        acts[:, cols], right[...], (((0,), (0,)), ((), ())), preferred_element_type=F32
    )


def kernel(
    a_hbm,
    g_hbm,
    gp_hbm,
    up_hbm,
    gu_hbm,
    dn_hbm,
    gi_hbm,
    wg_out,
    wd_out,
    gb,
    ab,
    wd,
    wg,
    gpt,
    upt,
    ghf,
    ghs,
    ghr,
    silu_s,
    dgate_s,
    hid,
    ghb,
    dws_d,
    dwr_d,
    dws_g,
    dwr_g,
    vs_d,
    vs_g,
    r1_d,
    r1_g,
    r2_d,
    r2_g,
    pb,
    r1p,
    r1m,
    r2p,
    r2m,
    yb,
    zr,
    ob,
    lsem,
    ss,
    rs,
):
    l, x, c, h, y = (lax.axis_index(n) for n in (Z, X, C, H, Y))
    xp, xm, xo = (x + 1) % 4, (x + 3) % 4, (x + 2) % 4
    yp, ym, yo = (y + 1) % 4, (y + 3) % 4, (y + 2) % 4
    to_xp, to_xm = {X: xp}, {X: xm}
    to_yp, to_ym = {Y: yp}, {Y: ym}
    sib = {C: 1 - c}
    inner = {Z: 1 - l}
    outer = {Z: 1 - l, H: (h + 2 * l + 3) % 4}
    z = 2 * h + l
    zpeers = [{Z: (z + j) % 2, H: ((z + j) % 8) // 2} for j in range(1, 8)]
    hpeers = [{H: (h + j) % 4} for j in range(1, 4)]
    sems = Sems()
    sent = []

    def copy(src, dst, sem, to):
        return pltpu.make_async_remote_copy(
            src_ref=src,
            dst_ref=dst,
            send_sem=ss.at[sem],
            recv_sem=rs.at[sem],
            device_id=to,
            device_id_type=pl.DeviceIdType.MESH,
        )

    def send(src, dst, sem, to):
        made = copy(src, dst, sem, to)
        made.start()
        sent.append(made)

    def got(dst, sem):
        copy(dst, dst, sem, sib).wait_recv()

    mine = pl.ds(pl.multiple_of(l * TOK, TOK), TOK)
    theirs = pl.ds(pl.multiple_of((1 - l) * TOK, TOK), TOK)
    my_cols = pl.ds(pl.multiple_of(l * DH, 128), DH)
    their_cols = pl.ds(pl.multiple_of((1 - l) * DH, 128), DH)

    def slab_rows(xs, core, part=None):
        start = xs * SLAB + core * ROWS
        if part is None:
            return pl.ds(pl.multiple_of(start, 32), ROWS)
        return pl.ds(pl.multiple_of(start + part * HALF, 32), HALF)

    own_rows = slab_rows(x, c)
    loads = [
        pltpu.make_async_copy(dn_hbm, wd.at[own_rows, :], lsem.at[0]),
        pltpu.make_async_copy(gp_hbm, gpt.at[l], lsem.at[1]),
        pltpu.make_async_copy(up_hbm, upt.at[l], lsem.at[2]),
        pltpu.make_async_copy(gu_hbm, wg.at[own_rows, :], lsem.at[3]),
        pltpu.make_async_copy(g_hbm.at[:, my_cols], gb.at[mine, :], lsem.at[4]),
        pltpu.make_async_copy(a_hbm.at[:, my_cols], ab.at[mine, :], lsem.at[5]),
    ]
    for load in loads:
        load.start()

    barrier = pltpu.get_barrier_semaphore()
    greeted = [to_xp, to_xm, to_yp, to_ym, sib] + zpeers
    for peer in greeted:
        pl.semaphore_signal(barrier, inc=1, device_id=peer, device_id_type=pl.DeviceIdType.MESH)
    pl.semaphore_wait(barrier, len(greeted))

    class Weights:
        def __init__(self, ref):
            self.ref = ref
            self.plus = sems.block(3)
            self.minus = sems.block(3)
            self.side = sems.block(4)

        def put(self, rows, sem, to):
            send(self.ref.at[rows, :], self.ref.at[rows, :], sem, to)

        def open(self):
            self.put(slab_rows(x, c, 0), self.plus, to_xp)
            self.put(slab_rows(x, c, 1), self.minus, to_xm)
            self.put(slab_rows(x, c, 1), self.plus + 1, to_xp)
            self.put(slab_rows(x, c, 0), self.minus + 1, to_xm)
            self.put(own_rows, self.side, sib)

        def forward(self):
            got(self.ref.at[slab_rows(xm, c, 0), :], self.plus)
            self.put(slab_rows(xm, c, 0), self.plus + 2, to_xp)
            got(self.ref.at[slab_rows(xp, c, 1), :], self.minus)
            self.put(slab_rows(xp, c, 1), self.minus + 2, to_xm)

        def near(self):
            got(self.ref.at[slab_rows(xm, c, 1), :], self.plus + 1)
            self.put(slab_rows(xm, c), self.side + 1, sib)
            got(self.ref.at[slab_rows(xp, c, 0), :], self.minus + 1)
            self.put(slab_rows(xp, c), self.side + 2, sib)

        def far(self):
            got(self.ref.at[slab_rows(xo, c, 0), :], self.plus + 2)
            got(self.ref.at[slab_rows(xo, c, 1), :], self.minus + 2)
            self.put(slab_rows(xo, c), self.side + 3, sib)

        def side_got(self, k):
            got(self.ref.at[slab_rows((x, xm, xp, xo)[k], 1 - c), :], self.side + k)

    class Tokens:
        def __init__(self, ref):
            self.ref = ref
            self.over = sems.block(2)
            self.plus = sems.block(3)
            self.minus = sems.block(3)

        def at(self, group, quarter, part=None):
            start = group * TOK + quarter * QT
            if part is None:
                return self.ref.at[pl.ds(pl.multiple_of(start, 32), QT), :]
            return self.ref.at[pl.ds(pl.multiple_of(start + part * 32, 32), 32), :]

        def open(self, hbm, ways):
            for part, way in enumerate(ways):
                rows = pl.ds(pl.multiple_of(y * QT + part * 32, 32), 32)
                send(hbm.at[rows, their_cols], self.at(l, y, part), self.over + part, way)

        def spread(self):
            for part, (first, second) in enumerate(
                (((self.plus, to_yp), (self.minus + 1, to_ym)), ((self.minus, to_ym), (self.plus + 1, to_yp)))
            ):
                piece = self.at(1 - l, y, part)
                got(piece, self.over + part)
                send(piece, piece, *first)
                send(piece, piece, *second)

        def forward(self):
            piece = self.at(1 - l, ym, 0)
            got(piece, self.plus)
            send(piece, piece, self.plus + 2, to_yp)
            piece = self.at(1 - l, yp, 1)
            got(piece, self.minus)
            send(piece, piece, self.minus + 2, to_ym)

        def near_got(self):
            got(self.at(1 - l, ym, 1), self.plus + 1)
            got(self.at(1 - l, yp, 0), self.minus + 1)

        def far_got(self):
            got(self.at(1 - l, yo, 0), self.plus + 2)
            got(self.at(1 - l, yo, 1), self.minus + 2)

    down, gate_up = Weights(wd), Weights(wg)
    outs, acts = Tokens(gb), Tokens(ab)

    outs.open(g_hbm, (inner, outer))
    loads[0].wait()
    down.open()
    acts.open(a_hbm, (outer, outer))
    loads[1].wait()
    loads[2].wait()
    pre_sem = sems.block(2)
    send(gpt.at[l], gpt.at[l], pre_sem, inner)
    send(upt.at[l], upt.at[l], pre_sem + 1, inner)
    loads[3].wait()
    gate_up.open()

    outs.spread()
    down.forward()
    acts.spread()
    down.near()

    def factors(group, rows):
        gate = jnp.transpose(gpt[group].astype(F32))
        up = jnp.transpose(upt[group].astype(F32))
        sig = jax.nn.sigmoid(gate)
        silu = gate * sig
        silu_s[rows, :] = silu
        dgate_s[rows, :] = up * sig * (1.0 + gate * (1.0 - sig))
        hid[rows, :] = (silu * up).astype(BF)

    factors(l, mine)
    outs.forward()
    down.far()
    for k in range(4):
        down.side_got(k)
    loads[4].wait()

    part = jnp.dot(gb[mine, :], wd[...], preferred_element_type=F32)
    ghf[mine, :] = part
    ghs[mine, :] = part.astype(BF)
    own_sem = sems.block(1)
    send(ghs.at[mine, :], ghr.at[mine, :], own_sem, inner)

    gate_up.forward()
    acts.forward()
    got(gpt.at[1 - l], pre_sem)
    got(upt.at[1 - l], pre_sem + 1)
    factors(1 - l, theirs)

    quarter_sem = sems.block(4)
    quarters = (y, ym, yp, yo)

    def quarter_rows(group, k):
        return pl.ds(pl.multiple_of(group * TOK + quarters[k] * QT, QT), QT)

    for k in range(4):
        if k == 1:
            outs.near_got()
        if k == 3:
            outs.far_got()
        rows = quarter_rows(1 - l, k)
        part = jnp.dot(gb[rows, :], wd[...], preferred_element_type=F32)
        ghf[rows, :] = part
        ghs[rows, :] = part.astype(BF)
        send(ghs.at[rows, :], ghr.at[rows, :], quarter_sem + k, inner)

    gate_up.near()

    order = (xo, xp, xm, x)

    def own(core):
        return pl.ds(pl.multiple_of(core * ROWS, 32), ROWS)

    class Grad:
        def __init__(self, left, right, mat, recv, pair, near1, near2, out):
            self.left, self.right = left, right
            self.mat, self.recv, self.pair = mat, recv, pair
            self.near1, self.near2, self.out = near1, near2, out
            self.cross = sems.block(4)
            self.plus = sems.block(3)
            self.minus = sems.block(3)

        def multiply(self, k):
            xs = order[k]
            self.mat[k] = wgrad_slab(self.left, self.right, xs).astype(BF)
            send(self.mat.at[k, own(1 - c), :], self.recv.at[k], self.cross + k, sib)

        def pair_sum(self, k):
            got(self.recv.at[k], self.cross + k)
            return self.mat[k, own(c), :].astype(F32) + self.recv[k].astype(F32)

        def start(self):
            lo, hi = pl.ds(0, HALF), pl.ds(HALF, HALF)
            self.pair[0] = self.pair_sum(0).astype(BF)
            send(self.pair.at[0, lo, :], self.near1.at[0], self.plus, to_xp)
            send(self.pair.at[0, hi, :], self.near1.at[1], self.minus, to_xm)
            self.pair[1] = self.pair_sum(1).astype(BF)
            send(self.pair.at[1, hi, :], self.near2.at[0, hi, :], self.plus + 1, to_xp)
            self.pair[2] = self.pair_sum(2).astype(BF)
            send(self.pair.at[2, lo, :], self.near2.at[1, lo, :], self.minus + 1, to_xm)

        def relay(self):
            lo, hi = pl.ds(0, HALF), pl.ds(HALF, HALF)
            got(self.near1.at[0], self.plus)
            self.pair[1, lo, :] = (self.pair[1, lo, :].astype(F32) + self.near1[0].astype(F32)).astype(BF)
            send(self.pair.at[1, lo, :], self.near2.at[0, lo, :], self.plus + 2, to_xp)
            got(self.near1.at[1], self.minus)
            self.pair[2, hi, :] = (self.pair[2, hi, :].astype(F32) + self.near1[1].astype(F32)).astype(BF)
            send(self.pair.at[2, hi, :], self.near2.at[1, hi, :], self.minus + 2, to_xm)

        def finish(self):
            lo, hi = pl.ds(0, HALF), pl.ds(HALF, HALF)
            total = self.pair_sum(3)
            got(self.near2.at[0, hi, :], self.plus + 1)
            got(self.near2.at[0, lo, :], self.plus + 2)
            got(self.near2.at[1, lo, :], self.minus + 1)
            got(self.near2.at[1, hi, :], self.minus + 2)
            total = total + self.near2[0].astype(F32) + self.near2[1].astype(F32)
            self.out[...] = total * (1.0 / 16.0)

    grad_down = Grad(gb, hid, dws_d, dwr_d, vs_d, r1_d, r2_d, wd_out)
    grad_gate = Grad(ab, ghb, dws_g, dwr_g, vs_g, r1_g, r2_g, wg_out)

    for k in range(4):
        grad_down.multiply(k)
        if k == 1:
            gate_up.far()
        if k == 2:
            grad_down.start()

    def hidden_grads(rows):
        total = ghf[rows, :] + ghr[rows, :].astype(F32)
        ghb[rows, pl.ds(0, FD)] = (total * dgate_s[rows, :]).astype(BF)
        ghb[rows, pl.ds(FD, FD)] = (total * silu_s[rows, :]).astype(BF)

    got(ghr.at[theirs, :], own_sem)
    hidden_grads(theirs)
    for k in range(4):
        rows = quarter_rows(l, k)
        got(ghr.at[rows, :], quarter_sem + k)
        hidden_grads(rows)

    for k in range(4):
        gate_up.side_got(k)

    slabs = (x, xm, xp, xo)
    y_rs = [sems.block(6) for _ in range(4)]
    z_rs = [sems.block(7) for _ in range(4)]
    z_ag = [sems.block(3) for _ in range(4)]
    y_ag = [sems.block(6) for _ in range(4)]
    stores = []

    def add_to(ref, other):
        ref[...] = (ref[...].astype(F32) + other[...].astype(F32)).astype(BF)

    def stage0(q):
        rows = pl.ds(pl.multiple_of(slabs[q] * SLAB, 128), SLAB)
        prod = lax.dot_general(
            ghb[...], wg[rows, :], (((1,), (1,)), ((), ())), preferred_element_type=F32
        )
        pb[q] = prod.astype(BF).reshape(2, 4, QT, SLAB)
        s = y_rs[q]
        send(pb.at[q, 0, yo], r1p.at[q], s, to_yp)
        send(pb.at[q, 1, yo], r1m.at[q], s + 1, to_ym)
        send(pb.at[q, 1, yp], r2p.at[q, 1], s + 2, to_yp)
        send(pb.at[q, 0, ym], r2m.at[q, 0], s + 3, to_ym)

    def stage1(q):
        s = y_rs[q]
        got(r1p.at[q], s)
        add_to(pb.at[q, 0, yp], r1p.at[q])
        send(pb.at[q, 0, yp], r2p.at[q, 0], s + 4, to_yp)
        got(r1m.at[q], s + 1)
        add_to(pb.at[q, 1, ym], r1m.at[q])
        send(pb.at[q, 1, ym], r2m.at[q, 1], s + 5, to_ym)

    def stage2(q):
        s = y_rs[q]
        got(r2p.at[q, 1], s + 2)
        got(r2m.at[q, 0], s + 3)
        got(r2p.at[q, 0], s + 4)
        got(r2m.at[q, 1], s + 5)
        yb[q] = (
            pb[q, :, y].astype(F32) + r2p[q].astype(F32) + r2m[q].astype(F32)
        ).astype(BF)
        for j in range(1, 8):
            to = (z + j) % 8
            rows = pl.ds(pl.multiple_of((to // 2) * HT, HT), HT)
            send(yb.at[q, to % 2, rows, :], zr.at[q, j - 1], z_rs[q] + j - 1, zpeers[j - 1])

    def stage3(q):
        for j in range(7):
            got(zr.at[q, j], z_rs[q] + j)
        here = pl.ds(pl.multiple_of(h * HT, HT), HT)
        place = pl.ds(pl.multiple_of(y * QT + h * HT, HT), HT)
        same = yb[q, l, here, :].astype(F32)
        for j in (1, 3, 5):
            same = same + zr[q, j].astype(F32)
        other = zr[q, 0].astype(F32)
        for j in (2, 4, 6):
            other = other + zr[q, j].astype(F32)
        xs = slabs[q]
        ob[xs, l, place, :] = same.astype(BF)
        ob[xs, 1 - l, place, :] = other.astype(BF)
        for j in range(3):
            piece = ob.at[xs, :, place, :]
            send(piece, piece, z_ag[q] + j, hpeers[j])

    def quarter(q, half, which):
        return ob.at[slabs[q], half, pl.ds(pl.multiple_of(which * QT, QT), QT), :]

    def stage4(q):
        for j in range(3):
            rows = pl.ds(pl.multiple_of(y * QT + ((h + 3 - j) % 4) * HT, HT), HT)
            got(ob.at[slabs[q], :, rows, :], z_ag[q] + j)
        s = y_ag[q]
        send(quarter(q, 0, y), quarter(q, 0, y), s, to_yp)
        send(quarter(q, 1, y), quarter(q, 1, y), s + 1, to_ym)
        send(quarter(q, 1, y), quarter(q, 1, y), s + 2, to_yp)
        send(quarter(q, 0, y), quarter(q, 0, y), s + 3, to_ym)

    def stage5(q):
        s = y_ag[q]
        got(quarter(q, 0, ym), s)
        send(quarter(q, 0, ym), quarter(q, 0, ym), s + 4, to_yp)
        got(quarter(q, 1, yp), s + 1)
        send(quarter(q, 1, yp), quarter(q, 1, yp), s + 5, to_ym)

    def stage6(q):
        s = y_ag[q]
        got(quarter(q, 1, ym), s + 2)
        got(quarter(q, 0, yp), s + 3)
        got(quarter(q, 0, yo), s + 4)
        got(quarter(q, 1, yo), s + 5)
        for half in range(2):
            cols = pl.ds(pl.multiple_of(half * DH + slabs[q] * SLAB, 128), SLAB)
            store = pltpu.make_async_copy(ob.at[slabs[q], half], gi_hbm.at[:, cols], lsem.at[6 + 2 * q + half])
            store.start()
            stores.append(store)

    stages = (stage0, stage1, stage2, stage3, stage4, stage5, stage6)
    for tick in range(10):
        for s in range(6, -1, -1):
            if 0 <= tick - s < 4:
                stages[s](tick - s)
        if tick == 0:
            grad_down.relay()
            acts.near_got()
            acts.far_got()
            loads[5].wait()
            grad_gate.multiply(0)
            grad_gate.multiply(1)
        if tick == 1:
            grad_gate.multiply(2)
            grad_gate.start()
        if tick == 2:
            grad_gate.multiply(3)
        if tick == 4:
            grad_gate.relay()
        if tick == 5:
            grad_down.finish()
    grad_gate.finish()

    for store in stores:
        store.wait()
    for made in sent:
        made.wait_send()


def per_device(activations, grad_out, gate_pre, up_pre, gate_up, down_weight):
    joined = jnp.concatenate([gate_up[:, 0, :], gate_up[:, 1, :]], axis=1)
    hbm = pl.BlockSpec(memory_space=pl.ANY)
    vmem = pl.BlockSpec(memory_space=pltpu.VMEM)
    scratch = [
        pltpu.VMEM((2 * TOK, DH), BF),
        pltpu.VMEM((2 * TOK, DH), BF),
        pltpu.VMEM((DH, FD), BF),
        pltpu.VMEM((DH, FG), BF),
        pltpu.VMEM((2, FD, TOK), BF),
        pltpu.VMEM((2, FD, TOK), BF),
        pltpu.VMEM((2 * TOK, FD), F32),
        pltpu.VMEM((2 * TOK, FD), BF),
        pltpu.VMEM((2 * TOK, FD), BF),
        pltpu.VMEM((2 * TOK, FD), F32),
        pltpu.VMEM((2 * TOK, FD), F32),
        pltpu.VMEM((2 * TOK, FD), BF),
        pltpu.VMEM((2 * TOK, FG), BF),
        pltpu.VMEM((4, SLAB, FD), BF),
        pltpu.VMEM((4, ROWS, FD), BF),
        pltpu.VMEM((4, SLAB, FG), BF),
        pltpu.VMEM((4, ROWS, FG), BF),
        pltpu.VMEM((3, ROWS, FD), BF),
        pltpu.VMEM((3, ROWS, FG), BF),
        pltpu.VMEM((2, HALF, FD), BF),
        pltpu.VMEM((2, HALF, FG), BF),
        pltpu.VMEM((2, ROWS, FD), BF),
        pltpu.VMEM((2, ROWS, FG), BF),
        pltpu.VMEM((4, 2, 4, QT, SLAB), BF),
        pltpu.VMEM((4, QT, SLAB), BF),
        pltpu.VMEM((4, QT, SLAB), BF),
        pltpu.VMEM((4, 2, QT, SLAB), BF),
        pltpu.VMEM((4, 2, QT, SLAB), BF),
        pltpu.VMEM((4, 2, QT, SLAB), BF),
        pltpu.VMEM((4, 7, HT, SLAB), BF),
        pltpu.VMEM((4, 2, TOK, SLAB), BF),
        pltpu.SemaphoreType.DMA((14,)),
        pltpu.SemaphoreType.DMA((160,)),
        pltpu.SemaphoreType.DMA((160,)),
    ]
    grad_input, gate_grad, down_grad = pl.pallas_call(
        kernel,
        out_shape=(
            jax.ShapeDtypeStruct((TOK, D), BF),
            jax.ShapeDtypeStruct((ROWS, FG), F32),
            jax.ShapeDtypeStruct((ROWS, FD), F32),
        ),
        in_specs=[hbm] * 6,
        out_specs=(hbm, vmem, vmem),
        scratch_shapes=scratch,
        compiler_params=pltpu.CompilerParams(
            collective_id=0, has_side_effects=True, vmem_limit_bytes=63 * 1024 * 1024
        ),
    )(activations, grad_out, gate_pre.T, up_pre.T, joined, down_weight)
    return grad_input, gate_grad.reshape(ROWS, 2, FD), down_grad


def solution(mesh):
    split = Mesh(mesh.devices.reshape(2, 4, 2, 4, 4), (Z, X, C, H, Y))
    return jax.shard_map(
        per_device,
        mesh=split,
        in_specs=(
            P(DP, None),
            P(DP, None),
            P(DP, TENSOR),
            P(DP, TENSOR),
            P(DP, None, TENSOR),
            P(DP, TENSOR),
        ),
        out_specs=(P(DP, None), P(DP, None, TENSOR), P(DP, TENSOR)),
        check_vma=False,
    )
```

time: 288 us -> 125 us (0.43)
  waiting for transfers between devices: 158 us -> 0 us
  Pallas kernels: 0 us -> 113 us
  matrix products: 28 us -> 0 us
  local copies, waits for them, and re-layouts: 36.9 us -> 10.4 us
  other arithmetic: 25.3 us -> 0.99 us
  blocking collectives: 18.7 us -> 0 us
  between operations: 13.9 us -> 0.65 us
  starting transfers between devices: 5.22 us -> 0 us
    pallas_call x0 -> x1, Pallas kernels: none -> 113 us  [per_device(): pl.pallas_call(kernel, out_shape=(jax.ShapeDtypeStruct((TOK, D), BF), jax...]
    all_gather x3 -> x0, waiting for transfers between devices: 80 us -> none  [the longest x1 48.5 us: per_device(): lax.all_gather(share_block.astype(jnp.bfloat16), TENSOR, axis=0, tiled=True)]
    reduce_scatter x2 -> x0, waiting for transfers between devices: 72.4 us -> none  [sum_in_order(): pieces = lax.psum_scatter(pieces, axes[k], scatter_dimension=0, tiled=True)]
    dot_general x4 -> x0, matrix products: 28 us -> none  [the longest x1 11.1 us: per_device(): lax.dot_general(grad_hidden, flattened, (((1,), (1,)), ((), ())), preferr...]
    dot_general x2 -> x0, local copies, waits for them, and re-layouts: 20.6 us -> none  [the longest x1 12.9 us: per_device(): lax.dot_general(activations, grad_hidden, (((0,), (0,)), ((), ())), prefe...]
    all_to_all x1 -> x0, blocking collectives: 18.7 us -> none  [sum_at_owner(): pieces = lax.all_to_all(split_up(x, dim, devices), axis, 0, 0, tiled=True)]
    reduce_sum x2 -> x0, other arithmetic: 17.4 us -> none  [the longest x1 13.1 us: sum_at_owner(): return jnp.sum(pieces.astype(jnp.float32), axis=0)]
    transpose x1 -> x0, other arithmetic: 7.72 us -> none  [split_up(): return jnp.moveaxis(pieces, dim, 0)]
  transfers between devices with their start and end apart: 6 -> 0, of which waited for: 5 -> 0; matrix products, arithmetic and copies ran while one was open for 30% -> 0% of each run, Pallas kernels for 0% -> 0%
where the time goes in v1:
time: 125 us
  Pallas kernels  113 us (90%)
  local copies, waits for them, and re-layouts  10.4 us (8%)
    pallas_call x1, Pallas kernels, per_device(): pl.pallas_call(kernel, out_shape=(jax.ShapeDtypeStruct((TOK, D), BF), jax...  113 us
    unnamed x4, local copies, waits for them, and re-layouts  4.31 us
    reshape x1, local copies, waits for them, and re-layouts, per_device(): return (grad_input, gate_grad.reshape(ROWS, 2, FD), down_grad)  3.53 us

profile of v1, /device:TPU:8, one launch (start us, length us, event | category | flops | bytes accessed | tf_op | source)
XLA Modules:
  0.0 124.8 jit_solution(183644791800412528)
XLA Ops:
  0.6 2.4 %fusion = (bf16[320,1,448]{2,1,0:T(2,128)(2,1)S(1)}, bf16[320,1,448]{2,1,0:T(2,128)(2,1)S(1)}) fusion(bf16[320,2,448]{2,1,0:T(2,128)(2,1)} %param.10), kind=kLoop, calls=%fused_computation.3 | loop fusion | bytes 1146880 | tf_op jit(solution)/shard_map/slice | solution.py:499
  3.1 0.2 copy_bitcast_fusion
  3.2 1.0 pad_maximum_fusion.gu_hbm
  4.2 112.7 %shard_map.85 = (bf16[256,5120]{1,0:T(8,128)(2,1)}, f32[320,896]{1,0:T(8,128)}, f32[320,448]{1,0:T(8,128)}) custom-call(bf16[256,5120]{1,0:T(8,128)(2,1)} %a_hbm.1, bf16[256,5120]{1,0:T(8,128)(2,1)} %g_hbm.1, bf16[448,256]{1,0:T(8,128)(2,1)} %bitcast.6, bf16[448,256]{1,0:T(8,128)(2,1)} %bitcast.7, bf16[320,896]{1,0:T(8,128)(2,1)} %pad_maximum_fusion.gu_hbm, ...), custom_call_target="tpu_custom_call" | custom-call | tf_op jit(solution)/shard_map/pallas_call | solution.py:538
  117.0 3.5 %reshape.9 = f32[320,2,448]{2,1,0:T(2,128)} reshape(f32[320,896]{1,0:T(8,128)} %get-tuple-element.7) | data formatting | bytes 2293760 | tf_op jit(solution)/shard_map/reshape | solution.py:552
  120.5 0.0 copy-start
  120.5 3.5 %copy.17 = bf16[256,5120]{1,0:T(8,128)(2,1)} copy(bf16[256,5120]{1,0:T(8,128)(2,1)} %get-tuple-element.16) | data formatting | bytes 5242880
  124.0 0.0 copy-done
  124.0 0.8 copy.18
Async XLA Ops:
  120.5 3.5 %copy-start = (f32[320,448]{1,0:T(8,128)S(1)}, f32[320,448]{1,0:T(8,128)}, u32[]{:S(2)}) copy-start(f32[320,448]{1,0:T(8,128)} %get-tuple-element.18) | copy-start | bytes 1720324

commit v2 on v1

v2 whole, which is shorter than its diff:
```python
import jax
import jax.numpy as jnp
from jax import lax
from jax.experimental import pallas as pl
from jax.experimental.pallas import tpu as pltpu
from jax.sharding import Mesh
from jax.sharding import PartitionSpec as P

Z, X, C, H, Y = "dp_0", "dp_1", "dp_2", "tensor_0", "tensor_1"
DP = (Z, X, C)
TENSOR = (H, Y)
BF = jnp.bfloat16
F32 = jnp.float32

TOK = 256
D = 5120
DH = D // 2
SLAB = 640
ROWS = 320
HALF = 160
FD = 448
FG = 896
QT = 64
HT = 16


class Sems:
    def __init__(self):
        self.n = 0

    def block(self, count=1):
        first = self.n
        self.n += count
        return first


def wgrad_slab(acts, right, xs):
    cols = pl.ds(pl.multiple_of(xs * SLAB, 128), SLAB)
    return lax.dot_general(
        acts[:, cols], right[...], (((0,), (0,)), ((), ())), preferred_element_type=F32
    )


def kernel(
    a_hbm,
    g_hbm,
    gp_hbm,
    up_hbm,
    gu_hbm,
    dn_hbm,
    ob,
    wg_out,
    wd_out,
    gu3,
    gb,
    ab,
    wd,
    wg,
    gpt,
    upt,
    ghf,
    ghs,
    ghr,
    silu_s,
    dgate_s,
    hid,
    ghb,
    dws_d,
    dwr_d,
    dws_g,
    dwr_g,
    vs_d,
    vs_g,
    r1_d,
    r1_g,
    r2_d,
    r2_g,
    pb,
    r1,
    r2,
    r3,
    yb,
    zr,
    lsem,
    ss,
    rs,
):
    l, x, c, h, y = (lax.axis_index(n) for n in (Z, X, C, H, Y))
    xp, xm, xo = (x + 1) % 4, (x + 3) % 4, (x + 2) % 4
    yp, ym, yo = (y + 1) % 4, (y + 3) % 4, (y + 2) % 4
    to_xp, to_xm = {X: xp}, {X: xm}
    to_yp, to_ym = {Y: yp}, {Y: ym}
    hp, hm, ho = (h + 1) % 4, (h + 3) % 4, (h + 2) % 4
    sib = {C: 1 - c}
    inner = {Z: 1 - l}
    outer = {Z: 1 - l, H: (h + 2 * l + 3) % 4}
    cross = [{Z: 1 - l, H: (h + j) % 4} for j in range(4)]
    along = [None] + [{H: (h + j) % 4} for j in range(1, 4)]
    sems = Sems()
    sent = []

    def copy(src, dst, sem, to):
        return pltpu.make_async_remote_copy(
            src_ref=src,
            dst_ref=dst,
            send_sem=ss.at[sem],
            recv_sem=rs.at[sem],
            device_id=to,
            device_id_type=pl.DeviceIdType.MESH,
        )

    def send(src, dst, sem, to):
        made = copy(src, dst, sem, to)
        made.start()
        sent.append(made)

    def got(dst, sem):
        copy(dst, dst, sem, sib).wait_recv()

    mine = pl.ds(pl.multiple_of(l * TOK, TOK), TOK)
    theirs = pl.ds(pl.multiple_of((1 - l) * TOK, TOK), TOK)
    my_cols = pl.ds(pl.multiple_of(l * DH, 128), DH)
    their_cols = pl.ds(pl.multiple_of((1 - l) * DH, 128), DH)

    def slab_rows(xs, core, part=None):
        start = xs * SLAB + core * ROWS
        if part is None:
            return pl.ds(pl.multiple_of(start, 32), ROWS)
        return pl.ds(pl.multiple_of(start + part * HALF, 32), HALF)

    own_rows = slab_rows(x, c)
    loads = [
        pltpu.make_async_copy(dn_hbm, wd.at[own_rows, :], lsem.at[0]),
        pltpu.make_async_copy(gp_hbm, gpt.at[l], lsem.at[1]),
        pltpu.make_async_copy(up_hbm, upt.at[l], lsem.at[2]),
        pltpu.make_async_copy(gu_hbm, gu3, lsem.at[3]),
        pltpu.make_async_copy(g_hbm.at[:, my_cols], gb.at[mine, :], lsem.at[4]),
        pltpu.make_async_copy(a_hbm.at[:, my_cols], ab.at[mine, :], lsem.at[5]),
    ]
    for load in loads:
        load.start()
    loads[3].wait()
    wg[own_rows, :] = gu3[...].reshape(ROWS, FG)

    barrier = pltpu.get_barrier_semaphore()
    greeted = [to_xp, to_xm, to_yp, to_ym, sib] + cross + along[1:]
    for peer in greeted:
        pl.semaphore_signal(barrier, inc=1, device_id=peer, device_id_type=pl.DeviceIdType.MESH)
    pl.semaphore_wait(barrier, len(greeted))

    class Weights:
        def __init__(self, ref):
            self.ref = ref
            self.plus = sems.block(3)
            self.minus = sems.block(3)
            self.side = sems.block(4)

        def put(self, rows, sem, to):
            send(self.ref.at[rows, :], self.ref.at[rows, :], sem, to)

        def open(self):
            self.put(slab_rows(x, c, 0), self.plus, to_xp)
            self.put(slab_rows(x, c, 1), self.minus, to_xm)
            self.put(slab_rows(x, c, 1), self.plus + 1, to_xp)
            self.put(slab_rows(x, c, 0), self.minus + 1, to_xm)
            self.put(own_rows, self.side, sib)

        def forward(self):
            got(self.ref.at[slab_rows(xm, c, 0), :], self.plus)
            self.put(slab_rows(xm, c, 0), self.plus + 2, to_xp)
            got(self.ref.at[slab_rows(xp, c, 1), :], self.minus)
            self.put(slab_rows(xp, c, 1), self.minus + 2, to_xm)

        def near(self):
            got(self.ref.at[slab_rows(xm, c, 1), :], self.plus + 1)
            self.put(slab_rows(xm, c), self.side + 1, sib)
            got(self.ref.at[slab_rows(xp, c, 0), :], self.minus + 1)
            self.put(slab_rows(xp, c), self.side + 2, sib)

        def far(self):
            got(self.ref.at[slab_rows(xo, c, 0), :], self.plus + 2)
            got(self.ref.at[slab_rows(xo, c, 1), :], self.minus + 2)
            self.put(slab_rows(xo, c), self.side + 3, sib)

        def side_got(self, k):
            got(self.ref.at[slab_rows((x, xm, xp, xo)[k], 1 - c), :], self.side + k)

    class Tokens:
        def __init__(self, ref):
            self.ref = ref
            self.over = sems.block(2)
            self.plus = sems.block(3)
            self.minus = sems.block(3)

        def at(self, group, quarter, part=None):
            start = group * TOK + quarter * QT
            if part is None:
                return self.ref.at[pl.ds(pl.multiple_of(start, 32), QT), :]
            return self.ref.at[pl.ds(pl.multiple_of(start + part * 32, 32), 32), :]

        def open(self, hbm, way):
            for part in range(2):
                rows = pl.ds(pl.multiple_of(y * QT + part * 32, 32), 32)
                send(hbm.at[rows, their_cols], self.at(l, y, part), self.over + part, way)

        def spread(self, part):
            piece = self.at(1 - l, y, part)
            got(piece, self.over + part)
            if part == 0:
                send(piece, piece, self.plus, to_yp)
                send(piece, piece, self.minus + 1, to_ym)
            else:
                send(piece, piece, self.minus, to_ym)
                send(piece, piece, self.plus + 1, to_yp)

        def forward(self, part):
            if part == 0:
                piece = self.at(1 - l, ym, 0)
                got(piece, self.plus)
                send(piece, piece, self.plus + 2, to_yp)
            else:
                piece = self.at(1 - l, yp, 1)
                got(piece, self.minus)
                send(piece, piece, self.minus + 2, to_ym)

        def near_got(self):
            got(self.at(1 - l, ym, 1), self.plus + 1)
            got(self.at(1 - l, yp, 0), self.minus + 1)

        def far_got(self):
            got(self.at(1 - l, yo, 0), self.plus + 2)
            got(self.at(1 - l, yo, 1), self.minus + 2)

    down, gate_up = Weights(wd), Weights(wg)
    outs = Tokens(gb)
    acts_sem = sems.block(2)
    pre_sem = sems.block(2)
    own_sem = sems.block(1)
    quarter_sem = sems.block(4)
    quarters = (y, ym, yp, yo)

    def acts_rows(part):
        first, count = ((0, 192), (192, 64))[part]
        return pl.ds(first, count), pl.ds(pl.multiple_of(l * TOK + first, 64), count), pl.ds(
            pl.multiple_of((1 - l) * TOK + first, 64), count
        )

    def acts_send(part, way):
        here, there, _ = acts_rows(part)
        send(a_hbm.at[here, their_cols], ab.at[there, :], acts_sem + part, way)

    def acts_got():
        for part in range(2):
            got(ab.at[acts_rows(part)[2], :], acts_sem + part)
        loads[5].wait()

    def pre_open():
        loads[1].wait()
        loads[2].wait()
        send(gpt.at[l], gpt.at[l], pre_sem, inner)
        send(upt.at[l], upt.at[l], pre_sem + 1, inner)

    def factors(group, rows):
        gate = jnp.transpose(gpt[group].astype(F32))
        up = jnp.transpose(upt[group].astype(F32))
        sig = jax.nn.sigmoid(gate)
        silu = gate * sig
        silu_s[rows, :] = silu
        dgate_s[rows, :] = up * sig * (1.0 + gate * (1.0 - sig))
        hid[rows, :] = (silu * up).astype(BF)

    def their_factors():
        got(gpt.at[1 - l], pre_sem)
        got(upt.at[1 - l], pre_sem + 1)
        factors(1 - l, theirs)

    def product(rows, sem):
        part = jnp.dot(gb[rows, :], wd[...], preferred_element_type=F32)
        ghf[rows, :] = part
        ghs[rows, :] = part.astype(BF)
        send(ghs.at[rows, :], ghr.at[rows, :], sem, inner)

    def own_product():
        for k in range(4):
            down.side_got(k)
        loads[4].wait()
        product(mine, own_sem)

    def quarter_rows(group, k):
        return pl.ds(pl.multiple_of(group * TOK + quarters[k] * QT, QT), QT)

    def quarter_product(k):
        product(quarter_rows(1 - l, k), quarter_sem + k)

    def near_products():
        outs.near_got()
        quarter_product(1)
        quarter_product(2)

    def far_product():
        outs.far_got()
        quarter_product(3)
        acts_send(1, inner)

    order = (xo, xp, xm, x)

    def own(core):
        return pl.ds(pl.multiple_of(core * ROWS, 32), ROWS)

    class Grad:
        def __init__(self, left, right, mat, recv, pair, near1, near2, out):
            self.left, self.right = left, right
            self.mat, self.recv, self.pair = mat, recv, pair
            self.near1, self.near2, self.out = near1, near2, out
            self.cross = sems.block(4)
            self.plus = sems.block(3)
            self.minus = sems.block(3)

        def multiply(self, k):
            xs = order[k]
            self.mat[k] = wgrad_slab(self.left, self.right, xs).astype(BF)
            send(self.mat.at[k, own(1 - c), :], self.recv.at[k], self.cross + k, sib)

        def pair_sum(self, k):
            got(self.recv.at[k], self.cross + k)
            return self.mat[k, own(c), :].astype(F32) + self.recv[k].astype(F32)

        def start(self):
            lo, hi = pl.ds(0, HALF), pl.ds(HALF, HALF)
            self.pair[0] = self.pair_sum(0).astype(BF)
            send(self.pair.at[0, lo, :], self.near1.at[0], self.plus, to_xp)
            send(self.pair.at[0, hi, :], self.near1.at[1], self.minus, to_xm)
            self.pair[1] = self.pair_sum(1).astype(BF)
            send(self.pair.at[1, hi, :], self.near2.at[0, hi, :], self.plus + 1, to_xp)
            self.pair[2] = self.pair_sum(2).astype(BF)
            send(self.pair.at[2, lo, :], self.near2.at[1, lo, :], self.minus + 1, to_xm)

        def relay(self):
            lo, hi = pl.ds(0, HALF), pl.ds(HALF, HALF)
            got(self.near1.at[0], self.plus)
            self.pair[1, lo, :] = (self.pair[1, lo, :].astype(F32) + self.near1[0].astype(F32)).astype(BF)
            send(self.pair.at[1, lo, :], self.near2.at[0, lo, :], self.plus + 2, to_xp)
            got(self.near1.at[1], self.minus)
            self.pair[2, hi, :] = (self.pair[2, hi, :].astype(F32) + self.near1[1].astype(F32)).astype(BF)
            send(self.pair.at[2, hi, :], self.near2.at[1, hi, :], self.minus + 2, to_xm)

        def finish(self):
            lo, hi = pl.ds(0, HALF), pl.ds(HALF, HALF)
            total = self.pair_sum(3)
            got(self.near2.at[0, hi, :], self.plus + 1)
            got(self.near2.at[0, lo, :], self.plus + 2)
            got(self.near2.at[1, lo, :], self.minus + 1)
            got(self.near2.at[1, hi, :], self.minus + 2)
            total = total + self.near2[0].astype(F32) + self.near2[1].astype(F32)
            total = total * (1.0 / 16.0)
            if self.out.ndim == 3:
                self.out[:, 0, :] = total[:, :FD]
                self.out[:, 1, :] = total[:, FD:]
            else:
                self.out[...] = total

    grad_down = Grad(gb, hid, dws_d, dwr_d, vs_d, r1_d, r2_d, wd_out)
    grad_gate = Grad(ab, ghb, dws_g, dwr_g, vs_g, r1_g, r2_g, wg_out)

    def hidden_grads(rows):
        total = ghf[rows, :] + ghr[rows, :].astype(F32)
        ghb[rows, pl.ds(0, FD)] = (total * dgate_s[rows, :]).astype(BF)
        ghb[rows, pl.ds(FD, FD)] = (total * silu_s[rows, :]).astype(BF)

    def their_grads():
        got(ghr.at[theirs, :], own_sem)
        hidden_grads(theirs)

    def my_grads():
        for k in range(4):
            got(ghr.at[quarter_rows(l, k), :], quarter_sem + k)
        hidden_grads(mine)

    slabs = (x, xm, xp, xo)
    y_rs = [sems.block(3) for _ in range(8)]
    z_rs = [sems.block(4) for _ in range(8)]
    z_ag = [sems.block(3) for _ in range(8)]
    y_ag = [sems.block(3) for _ in range(8)]

    def ways(i):
        if i % 2 == 0:
            return (to_yp, yp), (to_ym, ym)
        return (to_ym, ym), (to_yp, yp)

    def stage0(i):
        s, kind = i // 2, i % 2
        if kind == 0 and s > 0:
            gate_up.side_got(s)
        if i == 0:
            gate_up.side_got(0)
        rows = pl.ds(pl.multiple_of(slabs[s] * SLAB, 128), SLAB)
        prod = lax.dot_general(
            ghb[theirs if kind == 0 else mine, :],
            wg[rows, :],
            (((1,), (1,)), ((), ())),
            preferred_element_type=F32,
        )
        pb[i] = prod.astype(BF).reshape(4, QT, SLAB)
        (ahead, _), (behind, behind_y) = ways(i)
        send(pb.at[i, yo], r1.at[i], y_rs[i], ahead)
        send(pb.at[i, behind_y], r3.at[i], y_rs[i] + 1, behind)

    def stage1(i):
        (ahead, ahead_y), _ = ways(i)
        got(r1.at[i], y_rs[i])
        pb[i, ahead_y] = (pb[i, ahead_y].astype(F32) + r1[i].astype(F32)).astype(BF)
        send(pb.at[i, ahead_y], r2.at[i], y_rs[i] + 2, ahead)

    def stage2(i):
        got(r3.at[i], y_rs[i] + 1)
        got(r2.at[i], y_rs[i] + 2)
        yb[i] = (pb[i, y].astype(F32) + r2[i].astype(F32) + r3[i].astype(F32)).astype(BF)
        for j in (2, 1, 3, 0):
            to = cross[j] if i % 2 == 0 else along[j]
            if to is not None:
                rows = pl.ds(pl.multiple_of(((h + j) % 4) * HT, HT), HT)
                send(yb.at[i, rows, :], zr.at[i, j], z_rs[i] + j, to)

    def z_piece(i, which):
        half = 1 - l if i % 2 == 0 else l
        return ob.at[slabs[i // 2], half, pl.ds(pl.multiple_of(y * QT + which * HT, HT), HT), :]

    def stage3(i):
        if i % 2 == 0:
            got(zr.at[i, 0], z_rs[i])
            total = zr[i, 0].astype(F32)
        else:
            total = yb[i, pl.ds(pl.multiple_of(h * HT, HT), HT), :].astype(F32)
        for j in range(1, 4):
            got(zr.at[i, j], z_rs[i] + j)
            total = total + zr[i, j].astype(F32)
        piece = z_piece(i, h)
        piece[...] = total.astype(BF)
        send(piece, piece, z_ag[i], along[1])
        send(piece, piece, z_ag[i] + 1, along[3])

    def stage4(i):
        behind, to = (hm, along[1]) if i % 2 == 0 else (hp, along[3])
        piece = z_piece(i, behind)
        got(piece, z_ag[i] + i % 2)
        send(piece, piece, z_ag[i] + 2, to)

    def quarter(i, which):
        half = 1 - l if i % 2 == 0 else l
        return ob.at[slabs[i // 2], half, pl.ds(pl.multiple_of(which * QT, QT), QT), :]

    def stage5(i):
        got(z_piece(i, hp if i % 2 == 0 else hm), z_ag[i] + 1 - i % 2)
        got(z_piece(i, ho), z_ag[i] + 2)
        (ahead, _), (behind, _) = ways(i)
        send(quarter(i, y), quarter(i, y), y_ag[i], ahead)
        send(quarter(i, y), quarter(i, y), y_ag[i] + 1, behind)

    def stage6(i):
        (ahead, _), (_, behind_y) = ways(i)
        got(quarter(i, behind_y), y_ag[i])
        send(quarter(i, behind_y), quarter(i, behind_y), y_ag[i] + 2, ahead)

    def stage7(i):
        (_, ahead_y), _ = ways(i)
        got(quarter(i, ahead_y), y_ag[i] + 1)
        got(quarter(i, yo), y_ag[i] + 2)

    plan = []

    def at(time, fn, *args):
        plan.append((time, len(plan), fn, args))

    at(0.0, outs.open, g_hbm, outer)
    at(0.1, loads[0].wait)
    at(0.2, down.open)
    at(0.3, pre_open)
    at(0.4, acts_send, 0, outer)
    at(0.5, factors, l, mine)
    at(5.4, down.forward)
    at(5.5, gate_up.open)
    at(6.3, outs.spread, 0)
    at(8.9, down.near)
    at(9.8, outs.spread, 1)
    at(11.5, outs.forward, 0)
    at(11.6, their_factors)
    at(12.2, down.far)
    at(13.8, own_product)
    at(14.8, quarter_product, 0)
    at(15.0, outs.forward, 1)
    at(15.6, near_products)
    at(18.3, gate_up.forward)
    at(20.2, far_product)
    for k in range(4):
        at(20.5 + 0.1 * k, grad_down.multiply, k)
    at(21.2, their_grads)
    at(24.0, my_grads)
    at(24.8, gate_up.near)
    at(23.9, grad_down.start)
    at(31.0, gate_up.far)
    at(34.5, grad_down.relay)
    at(33.0, acts_got)
    for k in range(4):
        at(33.1 + 0.9 * k, grad_gate.multiply, k)
    at(37.0, grad_gate.start)
    at(47.0, grad_gate.relay)
    at(46.0, grad_down.finish)
    at(59.0, grad_gate.finish)
    first = (21.5, 24.5, 26.4, 28.8, 31.5, 34.1, 36.7, 39.4)
    for i in range(8):
        time = first[i]
        at(time, stage0, i)
        at(time + 3.0, stage1, i)
        at(time + 6.0, stage2, i)
        at(time + 12.0, stage3, i)
        at(time + 15.5, stage4, i)
        time = max(time + 19.0, 42.0 + 2.6 * i)
        at(time, stage5, i)
        at(time + 3.5, stage6, i)
        at(time + 8.0, stage7, i)
    for time, _, fn, args in sorted(plan, key=lambda step: step[:2]):
        with jax.named_scope(getattr(fn, "__name__", "step") + "_".join([""] + [str(v) for v in args if isinstance(v, int)])):
            fn(*args)

    with jax.named_scope("sends"):
        for made in sent:
            made.wait_send()


def finish(ob, wg, wd, gi_hbm, wg_hbm, wd_hbm, sem):
    copies = [pltpu.make_async_copy(wg, wg_hbm, sem.at[8]), pltpu.make_async_copy(wd, wd_hbm, sem.at[9])]
    for k in range(8):
        cols = pl.ds((k % 2) * DH + (k // 2) * SLAB, SLAB)
        copies.append(pltpu.make_async_copy(ob.at[k // 2, k % 2], gi_hbm.at[:, cols], sem.at[k]))
    for made in copies:
        made.start()
    for made in copies:
        made.wait()


def per_device(activations, grad_out, gate_pre, up_pre, gate_up, down_weight):
    hbm = pl.BlockSpec(memory_space=pl.ANY)
    vmem = pl.BlockSpec(memory_space=pltpu.VMEM)
    scratch = [
        pltpu.VMEM((ROWS, 2, FD), BF),
        pltpu.VMEM((2 * TOK, DH), BF),
        pltpu.VMEM((2 * TOK, DH), BF),
        pltpu.VMEM((DH, FD), BF),
        pltpu.VMEM((DH, FG), BF),
        pltpu.VMEM((2, FD, TOK), BF),
        pltpu.VMEM((2, FD, TOK), BF),
        pltpu.VMEM((2 * TOK, FD), F32),
        pltpu.VMEM((2 * TOK, FD), BF),
        pltpu.VMEM((2 * TOK, FD), BF),
        pltpu.VMEM((2 * TOK, FD), F32),
        pltpu.VMEM((2 * TOK, FD), F32),
        pltpu.VMEM((2 * TOK, FD), BF),
        pltpu.VMEM((2 * TOK, FG), BF),
        pltpu.VMEM((4, SLAB, FD), BF),
        pltpu.VMEM((4, ROWS, FD), BF),
        pltpu.VMEM((4, SLAB, FG), BF),
        pltpu.VMEM((4, ROWS, FG), BF),
        pltpu.VMEM((3, ROWS, FD), BF),
        pltpu.VMEM((3, ROWS, FG), BF),
        pltpu.VMEM((2, HALF, FD), BF),
        pltpu.VMEM((2, HALF, FG), BF),
        pltpu.VMEM((2, ROWS, FD), BF),
        pltpu.VMEM((2, ROWS, FG), BF),
        pltpu.VMEM((8, 4, QT, SLAB), BF),
        pltpu.VMEM((8, QT, SLAB), BF),
        pltpu.VMEM((8, QT, SLAB), BF),
        pltpu.VMEM((8, QT, SLAB), BF),
        pltpu.VMEM((8, QT, SLAB), BF),
        pltpu.VMEM((8, 4, HT, SLAB), BF),
        pltpu.SemaphoreType.DMA((6,)),
        pltpu.SemaphoreType.DMA((170,)),
        pltpu.SemaphoreType.DMA((170,)),
    ]
    held = pl.pallas_call(
        kernel,
        out_shape=(
            pltpu.VMEM((4, 2, TOK, SLAB), BF),
            pltpu.VMEM((ROWS, 2, FD), F32),
            pltpu.VMEM((ROWS, FD), F32),
        ),
        in_specs=[hbm] * 6,
        out_specs=(vmem, vmem, vmem),
        scratch_shapes=scratch,
        compiler_params=pltpu.CompilerParams(
            collective_id=0, has_side_effects=True, vmem_limit_bytes=56 * 1024 * 1024
        ),
        name="step",
    )(activations, grad_out, gate_pre.T, up_pre.T, gate_up, down_weight)
    held = [pltpu.with_memory_space_constraint(v, pltpu.VMEM) for v in held]
    return pl.pallas_call(
        finish,
        out_shape=(
            jax.ShapeDtypeStruct((TOK, D), BF),
            jax.ShapeDtypeStruct((ROWS, 2, FD), F32),
            jax.ShapeDtypeStruct((ROWS, FD), F32),
        ),
        in_specs=[vmem] * 3,
        out_specs=(hbm, hbm, hbm),
        scratch_shapes=[pltpu.SemaphoreType.DMA((10,))],
        compiler_params=pltpu.CompilerParams(vmem_limit_bytes=4 * 1024 * 1024),
        name="finish",
    )(*held)


def solution(mesh):
    split = Mesh(mesh.devices.reshape(2, 4, 2, 4, 4), (Z, X, C, H, Y))
    return jax.shard_map(
        per_device,
        mesh=split,
        in_specs=(
            P(DP, None),
            P(DP, None),
            P(DP, TENSOR),
            P(DP, TENSOR),
            P(DP, None, TENSOR),
            P(DP, TENSOR),
        ),
        out_specs=(P(DP, None), P(DP, None, TENSOR), P(DP, TENSOR)),
        check_vma=False,
    )
```

time: 125 us -> 100 us (0.80)
  Pallas kernels: 113 us -> 99.6 us
  local copies, waits for them, and re-layouts: 10.4 us -> 0 us
    pallas_call x1 -> x2, Pallas kernels: 113 us -> 99.6 us  [the longest x1 97.3 us: per_device(): pl.pallas_call(kernel, out_shape=(pltpu.VMEM((4, 2, TOK, SLAB), BF), pltp...]
    unnamed x4 -> x0, local copies, waits for them, and re-layouts: 4.31 us -> none
    reshape x1 -> x0, local copies, waits for them, and re-layouts: 3.53 us -> none  [per_device(): return (grad_input, gate_grad.reshape(ROWS, 2, FD), down_grad)]
    slice x1 -> x0, local copies, waits for them, and re-layouts: 2.44 us -> none  [per_device(): joined = jnp.concatenate([gate_up[:, 0, :], gate_up[:, 1, :]], axis=1)]
where the time goes in v2:
time: 100 us
  Pallas kernels  99.6 us (100%)
    pallas_call x1, Pallas kernels, per_device(): pl.pallas_call(kernel, out_shape=(pltpu.VMEM((4, 2, TOK, SLAB), BF), pltp...  97.3 us
    pallas_call x1, Pallas kernels, per_device(): pl.pallas_call(finish, out_shape=(jax.ShapeDtypeStruct((TOK, D), BF), jax...  2.21 us

profile of v2, /device:TPU:8, one launch (start us, length us, event | category | flops | bytes accessed | tf_op | source)
XLA Modules:
  0.0 100.2 jit_solution(3724436276447603643)
XLA Ops:
  0.6 97.3 %step.1 = (bf16[4,2,256,640]{3,2,1,0:T(8,128)(2,1)S(1)}, f32[320,2,448]{2,1,0:T(2,128)S(1)}, f32[320,448]{1,0:T(8,128)S(1)}) custom-call(bf16[256,5120]{1,0:T(8,128)(2,1)} %a_hbm.1, bf16[256,5120]{1,0:T(8,128)(2,1)} %g_hbm.1, bf16[448,256]{1,0:T(8,128)(2,1)} %bitcast.2, bf16[448,256]{1,0:T(8,128)(2,1)} %bitcast.3, bf16[320,2,448]{2,1,0:T(2,128)(2,1)} %gu_hbm.1, ...), custom_call_target="tpu_custom_call" | custom-call | tf_op jit(solution)/shard_map/step/pallas_call | solution.py:579
  98.0 2.2 %finish.1 = (bf16[256,5120]{1,0:T(8,128)(2,1)}, f32[320,2,448]{2,1,0:T(2,128)}, f32[320,448]{1,0:T(8,128)}) custom-call(bf16[4,2,256,640]{3,2,1,0:T(8,128)(2,1)S(1)} %get-tuple-element.6.ob, f32[320,2,448]{2,1,0:T(2,128)S(1)} %get-tuple-element.7.wg, f32[320,448]{1,0:T(8,128)S(1)} %get-tuple-element.8.wd), custom_call_target="tpu_custom_call" | custom-call | tf_op jit(solution)/shard_map/finish/pallas_call | solution.py:595

commit v3 on v2

--- a/solution.py
+++ b/solution.py
@@ -22,6 +22,23 @@
 FG = 896
 QT = 64
 HT = 16
+
+CHUNKS = ((0, 0), (1, 0), (0, 1), (2, 0), (1, 1), (2, 1), (3, 0), (3, 1))
+DIRECT_SUM = (0, 1, 7)
+DIRECT_SPREAD = (0, 1, 6, 7)
+ORDER = (
+    "down.open", "outs.open", "pre_open", "down.forward", "spread_0", "down.near", "gate_up.open",
+    "acts_send_0", "spread_1", "down.far", "own_product", "quarter_product_0", "forward_0", "forward_1",
+    "their_factors", "gate_up.forward", "factors", "near_products", "far_product", "their_grads",
+    "gate_up.near", "s0_0", "dmul_0", "s1_0", "dmul_1", "s0_1", "my_grads", "s1_1", "s0_2", "s0_3", "dmul_2",
+    "s2_0", "s0_4", "gate_up.far", "grad_down.start", "s2_1", "gmul_0", "s1_2", "s0_5", "s3_0", "s1_3", "s3_1",
+    "s1_4", "s0_6", "gmul_1", "s2_2", "s4_0", "s1_5", "grad_down.relay", "s0_7", "s2_3", "gmul_2", "s2_4",
+    "s1_7", "s2_5", "s5_0", "dmul_3", "s3_3", "s1_6", "s4_1", "s5_1", "grad_gate.start", "s3_2", "s2_7", "s3_4",
+    "s4_3", "s4_2", "s3_5", "s2_6", "s6_1", "s6_0", "s5_3", "s4_4", "s5_2", "s4_5", "s3_7", "s3_6", "s5_4",
+    "s5_5", "s4_7", "gmul_3", "s5_7", "s4_6", "s5_6", "s6_3", "s6_2", "grad_gate.relay", "s6_4", "s6_5", "s6_6",
+    "s6_7", "s7_0", "s7_2", "grad_gate.finish", "s7_5", "s7_4", "s7_3", "grad_down.finish", "s7_1", "s7_6",
+    "s7_7",
+)
 
 
 class Sems:
@@ -259,6 +276,7 @@
         loads[2].wait()
         send(gpt.at[l], gpt.at[l], pre_sem, inner)
         send(upt.at[l], upt.at[l], pre_sem + 1, inner)
+        acts_send(1, inner)
 
     def factors(group, rows):
         gate = jnp.transpose(gpt[group].astype(F32))
@@ -300,7 +318,6 @@
     def far_product():
         outs.far_got()
         quarter_product(3)
-        acts_send(1, inner)
 
     order = (xo, xp, xm, x)
 
@@ -376,7 +393,8 @@
             got(ghr.at[quarter_rows(l, k), :], quarter_sem + k)
         hidden_grads(mine)
 
-    slabs = (x, xm, xp, xo)
+    slabs = [(x, xm, xp, xo)[k] for k, _ in CHUNKS]
+    kinds = [kind for _, kind in CHUNKS]
     y_rs = [sems.block(3) for _ in range(8)]
     z_rs = [sems.block(4) for _ in range(8)]
     z_ag = [sems.block(3) for _ in range(8)]
@@ -388,12 +406,10 @@
         return (to_ym, ym), (to_yp, yp)
 
     def stage0(i):
-        s, kind = i // 2, i % 2
-        if kind == 0 and s > 0:
-            gate_up.side_got(s)
-        if i == 0:
-            gate_up.side_got(0)
-        rows = pl.ds(pl.multiple_of(slabs[s] * SLAB, 128), SLAB)
+        k, kind = CHUNKS[i]
+        if all(CHUNKS[e][0] != k for e in range(i)):
+            gate_up.side_got(k)
+        rows = pl.ds(pl.multiple_of(slabs[i] * SLAB, 128), SLAB)
         prod = lax.dot_general(
             ghb[theirs if kind == 0 else mine, :],
             wg[rows, :],
@@ -401,32 +417,46 @@
             preferred_element_type=F32,
         )
         pb[i] = prod.astype(BF).reshape(4, QT, SLAB)
-        (ahead, _), (behind, behind_y) = ways(i)
-        send(pb.at[i, yo], r1.at[i], y_rs[i], ahead)
+        (ahead, ahead_y), (behind, behind_y) = ways(i)
+        send(pb.at[i, yo], r1.at[i], y_rs[i], {Y: yo} if i in DIRECT_SUM else ahead)
         send(pb.at[i, behind_y], r3.at[i], y_rs[i] + 1, behind)
+        if i in DIRECT_SUM:
+            send(pb.at[i, ahead_y], r2.at[i], y_rs[i] + 2, ahead)
 
     def stage1(i):
+        if i in DIRECT_SUM:
+            return
         (ahead, ahead_y), _ = ways(i)
         got(r1.at[i], y_rs[i])
         pb[i, ahead_y] = (pb[i, ahead_y].astype(F32) + r1[i].astype(F32)).astype(BF)
         send(pb.at[i, ahead_y], r2.at[i], y_rs[i] + 2, ahead)
 
     def stage2(i):
+        total = pb[i, y].astype(F32)
+        if i in DIRECT_SUM:
+            got(r1.at[i], y_rs[i])
+            total = total + r1[i].astype(F32)
         got(r3.at[i], y_rs[i] + 1)
         got(r2.at[i], y_rs[i] + 2)
-        yb[i] = (pb[i, y].astype(F32) + r2[i].astype(F32) + r3[i].astype(F32)).astype(BF)
+        yb[i] = (total + r2[i].astype(F32) + r3[i].astype(F32)).astype(BF)
         for j in (2, 1, 3, 0):
-            to = cross[j] if i % 2 == 0 else along[j]
+            to = cross[j] if kinds[i] == 0 else along[j]
             if to is not None:
                 rows = pl.ds(pl.multiple_of(((h + j) % 4) * HT, HT), HT)
                 send(yb.at[i, rows, :], zr.at[i, j], z_rs[i] + j, to)
 
+    def piece_of(i, first, count):
+        half = 1 - l if kinds[i] == 0 else l
+        return ob.at[slabs[i], half, pl.ds(pl.multiple_of(first, HT), count), :]
+
     def z_piece(i, which):
-        half = 1 - l if i % 2 == 0 else l
-        return ob.at[slabs[i // 2], half, pl.ds(pl.multiple_of(y * QT + which * HT, HT), HT), :]
+        return piece_of(i, y * QT + which * HT, HT)
+
+    def quarter(i, which):
+        return piece_of(i, which * QT, QT)
 
     def stage3(i):
-        if i % 2 == 0:
+        if kinds[i] == 0:
             got(zr.at[i, 0], z_rs[i])
             total = zr[i, 0].astype(F32)
         else:
@@ -436,21 +466,25 @@
             total = total + zr[i, j].astype(F32)
         piece = z_piece(i, h)
         piece[...] = total.astype(BF)
+        if i in DIRECT_SPREAD:
+            send(piece, piece, z_ag[i] + 2, along[2])
         send(piece, piece, z_ag[i], along[1])
         send(piece, piece, z_ag[i] + 1, along[3])
 
     def stage4(i):
+        if i in DIRECT_SPREAD:
+            return
         behind, to = (hm, along[1]) if i % 2 == 0 else (hp, along[3])
         piece = z_piece(i, behind)
         got(piece, z_ag[i] + i % 2)
         send(piece, piece, z_ag[i] + 2, to)
 
-    def quarter(i, which):
-        half = 1 - l if i % 2 == 0 else l
-        return ob.at[slabs[i // 2], half, pl.ds(pl.multiple_of(which * QT, QT), QT), :]
-
     def stage5(i):
-        got(z_piece(i, hp if i % 2 == 0 else hm), z_ag[i] + 1 - i % 2)
+        if i in DIRECT_SPREAD:
+            got(z_piece(i, hm), z_ag[i])
+            got(z_piece(i, hp), z_ag[i] + 1)
+        else:
+            got(z_piece(i, hp if i % 2 == 0 else hm), z_ag[i] + 1 - i % 2)
         got(z_piece(i, ho), z_ag[i] + 2)
         (ahead, _), (behind, _) = ways(i)
         send(quarter(i, y), quarter(i, y), y_ag[i], ahead)
@@ -466,61 +500,46 @@
         got(quarter(i, ahead_y), y_ag[i] + 1)
         got(quarter(i, yo), y_ag[i] + 2)
 
-    plan = []
-
-    def at(time, fn, *args):
-        plan.append((time, len(plan), fn, args))
-
-    at(0.0, outs.open, g_hbm, outer)
-    at(0.1, loads[0].wait)
-    at(0.2, down.open)
-    at(0.3, pre_open)
-    at(0.4, acts_send, 0, outer)
-    at(0.5, factors, l, mine)
-    at(5.4, down.forward)
-    at(5.5, gate_up.open)
-    at(6.3, outs.spread, 0)
-    at(8.9, down.near)
-    at(9.8, outs.spread, 1)
-    at(11.5, outs.forward, 0)
-    at(11.6, their_factors)
-    at(12.2, down.far)
-    at(13.8, own_product)
-    at(14.8, quarter_product, 0)
-    at(15.0, outs.forward, 1)
-    at(15.6, near_products)
-    at(18.3, gate_up.forward)
-    at(20.2, far_product)
-    for k in range(4):
-        at(20.5 + 0.1 * k, grad_down.multiply, k)
-    at(21.2, their_grads)
-    at(24.0, my_grads)
-    at(24.8, gate_up.near)
-    at(23.9, grad_down.start)
-    at(31.0, gate_up.far)
-    at(34.5, grad_down.relay)
-    at(33.0, acts_got)
-    for k in range(4):
-        at(33.1 + 0.9 * k, grad_gate.multiply, k)
-    at(37.0, grad_gate.start)
-    at(47.0, grad_gate.relay)
-    at(46.0, grad_down.finish)
-    at(59.0, grad_gate.finish)
-    first = (21.5, 24.5, 26.4, 28.8, 31.5, 34.1, 36.7, 39.4)
-    for i in range(8):
-        time = first[i]
-        at(time, stage0, i)
-        at(time + 3.0, stage1, i)
-        at(time + 6.0, stage2, i)
-        at(time + 12.0, stage3, i)
-        at(time + 15.5, stage4, i)
-        time = max(time + 19.0, 42.0 + 2.6 * i)
-        at(time, stage5, i)
-        at(time + 3.5, stage6, i)
-        at(time + 8.0, stage7, i)
-    for time, _, fn, args in sorted(plan, key=lambda step: step[:2]):
-        with jax.named_scope(getattr(fn, "__name__", "step") + "_".join([""] + [str(v) for v in args if isinstance(v, int)])):
-            fn(*args)
+    steps = {
+        "outs.open": lambda: outs.open(g_hbm, outer),
+        "down.open": lambda: (loads[0].wait(), down.open()),
+        "pre_open": pre_open,
+        "acts_send_0": lambda: acts_send(0, outer),
+        "factors": lambda: factors(l, mine),
+        "down.forward": down.forward,
+        "gate_up.open": gate_up.open,
+        "down.near": down.near,
+        "their_factors": their_factors,
+        "down.far": down.far,
+        "own_product": own_product,
+        "quarter_product_0": lambda: quarter_product(0),
+        "near_products": near_products,
+        "gate_up.forward": gate_up.forward,
+        "far_product": far_product,
+        "gate_up.near": gate_up.near,
+        "gate_up.far": gate_up.far,
+        "their_grads": their_grads,
+        "my_grads": my_grads,
+        "grad_down.start": grad_down.start,
+        "grad_down.relay": grad_down.relay,
+        "grad_down.finish": grad_down.finish,
+        "grad_gate.start": grad_gate.start,
+        "grad_gate.relay": grad_gate.relay,
+        "grad_gate.finish": grad_gate.finish,
+        "dmul": grad_down.multiply,
+        "gmul": lambda k: (acts_got() if k == 0 else None, grad_gate.multiply(k)),
+        "spread": outs.spread,
+        "forward": outs.forward,
+    }
+    for n, stage in enumerate((stage0, stage1, stage2, stage3, stage4, stage5, stage6, stage7)):
+        steps[f"s{n}"] = stage
+    for name in ORDER:
+        with jax.named_scope(name):
+            base, _, number = name.rpartition("_")
+            if name in steps:
+                steps[name]()
+            else:
+                steps[base](int(number))
 
     with jax.named_scope("sends"):
         for made in sent:

time: 100 us -> 92.6 us (0.926)
  Pallas kernels: 99.6 us -> 91.8 us
    pallas_call x1, Pallas kernels: 97.3 us -> 89.6 us  [per_device(): pl.pallas_call(kernel, out_shape=(pltpu.VMEM((4, 2, TOK, SLAB), BF), pltp...]
where the time goes in v3:
time: 92.6 us; the launch traced here: 92.5 us
  Pallas kernels  91.8 us (99%)
    pallas_call x1, Pallas kernels, per_device(): pl.pallas_call(kernel, out_shape=(pltpu.VMEM((4, 2, TOK, SLAB), BF), pltp...  89.6 us
    pallas_call x1, Pallas kernels, per_device(): pl.pallas_call(finish, out_shape=(jax.ShapeDtypeStruct((TOK, D), BF), jax...  2.21 us

profile of v3, /device:TPU:8, one launch (start us, length us, event | category | flops | bytes accessed | tf_op | source)
XLA Modules:
  0.0 92.5 jit_solution(6709232556779005388)
XLA Ops:
  0.6 89.6 %step.1 = (bf16[4,2,256,640]{3,2,1,0:T(8,128)(2,1)S(1)}, f32[320,2,448]{2,1,0:T(2,128)S(1)}, f32[320,448]{1,0:T(8,128)S(1)}) custom-call(bf16[256,5120]{1,0:T(8,128)(2,1)} %a_hbm.1, bf16[256,5120]{1,0:T(8,128)(2,1)} %g_hbm.1, bf16[448,256]{1,0:T(8,128)(2,1)} %bitcast.2, bf16[448,256]{1,0:T(8,128)(2,1)} %bitcast.3, bf16[320,2,448]{2,1,0:T(2,128)(2,1)} %gu_hbm.1, ...), custom_call_target="tpu_custom_call" | custom-call | tf_op jit(solution)/shard_map/step/pallas_call | solution.py:598
  90.3 2.2 %finish.1 = (bf16[256,5120]{1,0:T(8,128)(2,1)}, f32[320,2,448]{2,1,0:T(2,128)}, f32[320,448]{1,0:T(8,128)}) custom-call(bf16[4,2,256,640]{3,2,1,0:T(8,128)(2,1)S(1)} %get-tuple-element.6.ob, f32[320,2,448]{2,1,0:T(2,128)S(1)} %get-tuple-element.7.wg, f32[320,448]{1,0:T(8,128)S(1)} %get-tuple-element.8.wd), custom_call_target="tpu_custom_call" | custom-call | tf_op jit(solution)/shard_map/finish/pallas_call | solution.py:614

commit v4 on v3

v4 whole, which is shorter than its diff:
```python
import jax
import jax.numpy as jnp
from jax import lax
from jax.experimental import pallas as pl
from jax.experimental.pallas import tpu as pltpu
from jax.sharding import Mesh
from jax.sharding import PartitionSpec as P

Z, X, C, H, Y = "dp_0", "dp_1", "dp_2", "tensor_0", "tensor_1"
DP = (Z, X, C)
TENSOR = (H, Y)
BF = jnp.bfloat16
F32 = jnp.float32

TOK = 256
D = 5120
DH = D // 2
SLAB = 640
ROWS = 320
HALF = 160
FD = 448
FG = 896
QT = 64
HT = 16

OUTLETS, INLETS = 12, 88
CHUNKS = ((0, 0), (1, 0), (2, 0), (0, 1), (1, 1), (2, 1), (3, 0), (3, 1))
DIRECT_SUM = (0, 1)
DIRECT_SPREAD = (0, 1, 5, 6, 7)
ORDER = (
    1, 2, 0, 3, 6, 60, 4, 7, 8, 61, 10, 70, 5, 11, 71, 13, 14, 9, 12, 15, 18, 100, 16, 40, 41, 42, 101, 102, 19,
    43, 20, 17, 103, 104, 120, 50, 121, 51, 112, 105, 21, 130, 113, 114, 131, 106, 122, 115, 52, 123, 107, 22,
    124, 23, 116, 151, 132, 125, 117, 150, 133, 142, 134, 126, 143, 127, 161, 152, 144, 160, 135, 24, 136, 153,
    154, 137, 171, 155, 53, 156, 162, 164, 170, 157, 163, 25, 165, 166, 167, 173, 174, 175, 172, 177, 176,
)


class Sems:
    def __init__(self):
        self.n = 0

    def block(self, count=1):
        first = self.n
        self.n += count
        return first


def wgrad_slab(acts, right, xs):
    cols = pl.ds(pl.multiple_of(xs * SLAB, 128), SLAB)
    return lax.dot_general(
        acts[:, cols], right[...], (((0,), (0,)), ((), ())), preferred_element_type=F32
    )


def kernel(
    a_hbm,
    g_hbm,
    gp_hbm,
    up_hbm,
    gu_hbm,
    dn_hbm,
    ob,
    wg_out,
    wd_out,
    gu3,
    gb,
    ab,
    wd,
    wg,
    gpt,
    upt,
    ghf,
    ghs,
    ghr,
    silu_s,
    dgate_s,
    hid,
    ghb,
    dws_d,
    dwr_d,
    dws_g,
    dwr_g,
    vs_d,
    vs_g,
    r1_d,
    r1_g,
    r2_d,
    r2_g,
    pb,
    r1,
    r2,
    r3,
    yb,
    zr,
    lsem,
    ss,
    rs,
):
    l, x, c, h, y = (lax.axis_index(n) for n in (Z, X, C, H, Y))
    xp, xm, xo = (x + 1) % 4, (x + 3) % 4, (x + 2) % 4
    yp, ym, yo = (y + 1) % 4, (y + 3) % 4, (y + 2) % 4
    to_xp, to_xm = {X: xp}, {X: xm}
    to_yp, to_ym = {Y: yp}, {Y: ym}
    hp, hm, ho = (h + 1) % 4, (h + 3) % 4, (h + 2) % 4
    sib = {C: 1 - c}
    inner = {Z: 1 - l}
    outer = {Z: 1 - l, H: (h + 2 * l + 3) % 4}
    cross = [{Z: 1 - l, H: (h + j) % 4} for j in range(4)]
    along = [None] + [{H: (h + j) % 4} for j in range(1, 4)]
    sems, outlets = Sems(), Sems()

    def copy(src, dst, outlet, sem, to):
        return pltpu.make_async_remote_copy(
            src_ref=src,
            dst_ref=dst,
            send_sem=ss.at[outlet],
            recv_sem=rs.at[sem],
            device_id=to,
            device_id_type=pl.DeviceIdType.MESH,
        )

    def send(src, dst, outlet, sem, to):
        copy(src, dst, outlet, sem, to).start()

    def got(like, sem):
        copy(like, like, 0, sem, sib).wait_recv()

    def gone(like, outlet):
        copy(like, like, outlet, 0, sib).wait_send()

    mine = pl.ds(pl.multiple_of(l * TOK, TOK), TOK)
    theirs = pl.ds(pl.multiple_of((1 - l) * TOK, TOK), TOK)
    my_cols = pl.ds(pl.multiple_of(l * DH, 128), DH)
    their_cols = pl.ds(pl.multiple_of((1 - l) * DH, 128), DH)

    def slab_rows(xs, core, part=None):
        start = xs * SLAB + core * ROWS
        if part is None:
            return pl.ds(pl.multiple_of(start, 32), ROWS)
        return pl.ds(pl.multiple_of(start + part * HALF, 32), HALF)

    barrier = pltpu.get_barrier_semaphore()
    greeted = [to_xp, to_xm, to_yp, to_ym, sib] + cross + along[1:]
    for peer in greeted:
        pl.semaphore_signal(barrier, inc=1, device_id=peer, device_id_type=pl.DeviceIdType.MESH)

    own_rows = slab_rows(x, c)
    loads = [
        pltpu.make_async_copy(dn_hbm, wd.at[own_rows, :], lsem.at[0]),
        pltpu.make_async_copy(gp_hbm, gpt.at[l], lsem.at[1]),
        pltpu.make_async_copy(up_hbm, upt.at[l], lsem.at[2]),
        pltpu.make_async_copy(gu_hbm, gu3, lsem.at[3]),
        pltpu.make_async_copy(g_hbm.at[:, my_cols], gb.at[mine, :], lsem.at[4]),
        pltpu.make_async_copy(a_hbm.at[:, my_cols], ab.at[mine, :], lsem.at[5]),
    ]
    for load in loads:
        load.start()
    pl.semaphore_wait(barrier, len(greeted))

    class Weights:
        def __init__(self, ref):
            self.ref = ref
            self.outlet = outlets.block()
            self.first, self.second, self.last = sems.block(), sems.block(), sems.block()
            self.side = [sems.block() for _ in range(4)]

        def put(self, rows, sem, to):
            send(self.ref.at[rows, :], self.ref.at[rows, :], self.outlet, sem, to)

        def open(self):
            self.put(slab_rows(x, c, 0), self.first, to_xp)
            self.put(slab_rows(x, c, 1), self.first, to_xm)
            self.put(slab_rows(x, c, 1), self.second, to_xp)
            self.put(slab_rows(x, c, 0), self.second, to_xm)
            self.put(own_rows, self.side[0], sib)

        def forward(self):
            got(self.ref.at[pl.ds(0, ROWS), :], self.first)
            self.put(slab_rows(xm, c, 0), self.last, to_xp)
            self.put(slab_rows(xp, c, 1), self.last, to_xm)

        def near(self):
            got(self.ref.at[pl.ds(0, ROWS), :], self.second)
            self.put(slab_rows(xm, c), self.side[1], sib)
            self.put(slab_rows(xp, c), self.side[2], sib)

        def far(self):
            got(self.ref.at[pl.ds(0, ROWS), :], self.last)
            self.put(slab_rows(xo, c), self.side[3], sib)

        def side_got(self, k):
            got(self.ref.at[pl.ds(0, ROWS), :], self.side[k])

        def drain(self):
            gone(self.ref.at[pl.ds(0, 7 * ROWS), :], self.outlet)

    class Tokens:
        def __init__(self, ref):
            self.ref = ref
            self.outlet = outlets.block()
            self.over = sems.block(2)
            self.plus, self.minus = sems.block(), sems.block()
            self.near, self.far = sems.block(), sems.block()

        def at(self, group, quarter, part=None):
            start = group * TOK + quarter * QT
            if part is None:
                return self.ref.at[pl.ds(pl.multiple_of(start, 32), QT), :]
            return self.ref.at[pl.ds(pl.multiple_of(start + part * 32, 32), 32), :]

        def open(self, hbm, way):
            for part in range(2):
                rows = pl.ds(pl.multiple_of(y * QT + part * 32, 32), 32)
                send(hbm.at[rows, their_cols], self.at(l, y, part), self.outlet, self.over + part, way)

        def put(self, piece, sem, to):
            send(piece, piece, self.outlet, sem, to)

        def spread(self, part):
            piece = self.at(1 - l, y, part)
            got(piece, self.over + part)
            if part == 0:
                self.put(piece, self.plus, to_yp)
                self.put(piece, self.near, to_ym)
            else:
                self.put(piece, self.minus, to_ym)
                self.put(piece, self.near, to_yp)

        def forward(self, part):
            piece = self.at(1 - l, (ym, yp)[part], part)
            got(piece, (self.plus, self.minus)[part])
            self.put(piece, self.far, (to_yp, to_ym)[part])

        def near_got(self):
            got(self.ref.at[pl.ds(0, QT), :], self.near)

        def far_got(self):
            got(self.ref.at[pl.ds(0, QT), :], self.far)

    down, gate_up = Weights(wd), Weights(wg)
    outs = Tokens(gb)
    acts_sem, pre_sem, own_sem, quarter_sem = (sems.block() for _ in range(4))
    acts_out, pre_out, product_out = (outlets.block() for _ in range(3))
    quarters = (y, ym, yp, yo)

    def acts_rows(part):
        first, count = ((0, 192), (192, 64))[part]
        return pl.ds(first, count), pl.ds(pl.multiple_of(l * TOK + first, 64), count)

    def acts_send(part, way):
        here, there = acts_rows(part)
        send(a_hbm.at[here, their_cols], ab.at[there, :], acts_out, acts_sem, way)

    def acts_got():
        got(ab.at[pl.ds(0, TOK), :], acts_sem)
        loads[5].wait()

    def pre_open():
        loads[1].wait()
        loads[2].wait()
        send(gpt.at[l], gpt.at[l], pre_out, pre_sem, inner)
        send(upt.at[l], upt.at[l], pre_out, pre_sem, inner)
        acts_send(1, inner)

    def own_gate_up():
        loads[3].wait()
        wg[own_rows, :] = gu3[...].reshape(ROWS, FG)

    def factors(group, rows):
        gate = jnp.transpose(gpt[group].astype(F32))
        up = jnp.transpose(upt[group].astype(F32))
        sig = jax.nn.sigmoid(gate)
        silu = gate * sig
        silu_s[rows, :] = silu
        dgate_s[rows, :] = up * sig * (1.0 + gate * (1.0 - sig))
        hid[rows, :] = (silu * up).astype(BF)

    def their_factors():
        got(gpt, pre_sem)
        factors(1 - l, theirs)

    def product(rows, part, sem):
        ghf[rows, :] = part
        ghs[rows, :] = part.astype(BF)
        send(ghs.at[rows, :], ghr.at[rows, :], product_out, sem, inner)

    def slab_product(xs):
        where = pl.ds(pl.multiple_of(xs * SLAB, 128), SLAB)
        return jnp.dot(gb[mine, where], wd[where, :], preferred_element_type=F32)

    def own_product():
        loads[4].wait()
        for k in range(3):
            down.side_got(k)
        part = slab_product(x) + slab_product(xm) + slab_product(xp)
        down.side_got(3)
        product(mine, part + slab_product(xo), own_sem)

    def quarter_rows(group, k):
        return pl.ds(pl.multiple_of(group * TOK + quarters[k] * QT, QT), QT)

    def quarter_product(k):
        rows = quarter_rows(1 - l, k)
        product(rows, jnp.dot(gb[rows, :], wd[...], preferred_element_type=F32), quarter_sem)

    def near_products():
        outs.near_got()
        quarter_product(1)
        quarter_product(2)

    def far_product():
        outs.far_got()
        quarter_product(3)

    order = (xo, xp, xm, x)

    def own(core):
        return pl.ds(pl.multiple_of(core * ROWS, 32), ROWS)

    class Grad:
        def __init__(self, left, right, mat, recv, pair, near1, near2, out):
            self.left, self.right = left, right
            self.mat, self.recv, self.pair = mat, recv, pair
            self.near1, self.near2, self.out = near1, near2, out
            self.like = wd if right is hid else wg
            self.outlet = outlets.block()
            self.early, self.late, self.first, self.rest = (sems.block() for _ in range(4))

        def got(self, rows, sem):
            got(self.like.at[pl.ds(0, rows), :], sem)

        def put(self, src, dst, sem, to):
            send(src, dst, self.outlet, sem, to)

        def drain(self):
            gone(self.like.at[pl.ds(0, 7 * ROWS), :], self.outlet)

        def multiply(self, k):
            xs = order[k]
            self.mat[k] = wgrad_slab(self.left, self.right, xs).astype(BF)
            self.put(self.mat.at[k, own(1 - c), :], self.recv.at[k], self.late if k == 3 else self.early, sib)

        def pair_sum(self, k):
            return self.mat[k, own(c), :].astype(F32) + self.recv[k].astype(F32)

        def start(self):
            lo, hi = pl.ds(0, HALF), pl.ds(HALF, HALF)
            self.got(3 * ROWS, self.early)
            self.pair[0] = self.pair_sum(0).astype(BF)
            self.put(self.pair.at[0, lo, :], self.near1.at[0], self.first, to_xp)
            self.put(self.pair.at[0, hi, :], self.near1.at[1], self.first, to_xm)
            self.pair[1] = self.pair_sum(1).astype(BF)
            self.put(self.pair.at[1, hi, :], self.near2.at[0, hi, :], self.rest, to_xp)
            self.pair[2] = self.pair_sum(2).astype(BF)
            self.put(self.pair.at[2, lo, :], self.near2.at[1, lo, :], self.rest, to_xm)

        def relay(self):
            lo, hi = pl.ds(0, HALF), pl.ds(HALF, HALF)
            self.got(ROWS, self.first)
            self.pair[1, lo, :] = (self.pair[1, lo, :].astype(F32) + self.near1[0].astype(F32)).astype(BF)
            self.put(self.pair.at[1, lo, :], self.near2.at[0, lo, :], self.rest, to_xp)
            self.pair[2, hi, :] = (self.pair[2, hi, :].astype(F32) + self.near1[1].astype(F32)).astype(BF)
            self.put(self.pair.at[2, hi, :], self.near2.at[1, hi, :], self.rest, to_xm)

        def finish(self):
            self.got(ROWS, self.late)
            total = self.pair_sum(3)
            self.got(2 * ROWS, self.rest)
            total = total + self.near2[0].astype(F32) + self.near2[1].astype(F32)
            total = total * (1.0 / 16.0)
            if self.out.ndim == 3:
                self.out[:, 0, :] = total[:, :FD]
                self.out[:, 1, :] = total[:, FD:]
            else:
                self.out[...] = total

    grad_down = Grad(gb, hid, dws_d, dwr_d, vs_d, r1_d, r2_d, wd_out)
    grad_gate = Grad(ab, ghb, dws_g, dwr_g, vs_g, r1_g, r2_g, wg_out)

    def hidden_grads(rows):
        total = ghf[rows, :] + ghr[rows, :].astype(F32)
        ghb[rows, pl.ds(0, FD)] = (total * dgate_s[rows, :]).astype(BF)
        ghb[rows, pl.ds(FD, FD)] = (total * silu_s[rows, :]).astype(BF)

    def their_grads():
        got(ghr.at[theirs, :], own_sem)
        hidden_grads(theirs)

    def my_grads():
        got(ghr.at[mine, :], quarter_sem)
        hidden_grads(mine)

    slabs = [(x, xm, xp, xo)[k] for k, _ in CHUNKS]
    kinds = [kind for _, kind in CHUNKS]
    y_sum = [(sems.block(), sems.block()) for _ in range(8)]
    z_sum = [sems.block() for _ in range(8)]
    z_all = [(sems.block(), sems.block()) for _ in range(8)]
    y_all = [(sems.block(), sems.block()) for _ in range(8)]
    y_sum_out, z_sum_out, z_all_out, y_all_out = (outlets.block() for _ in range(4))

    def ways(i):
        if i % 2 == 0:
            return (to_yp, yp), (to_ym, ym)
        return (to_ym, ym), (to_yp, yp)

    def stage0(i):
        k, kind = CHUNKS[i]
        if all(CHUNKS[e][0] != k for e in range(i)):
            gate_up.side_got(k)
        rows = pl.ds(pl.multiple_of(slabs[i] * SLAB, 128), SLAB)
        prod = lax.dot_general(
            ghb[theirs if kind == 0 else mine, :],
            wg[rows, :],
            (((1,), (1,)), ((), ())),
            preferred_element_type=F32,
        )
        pb[i] = prod.astype(BF).reshape(4, QT, SLAB)
        (ahead, ahead_y), (behind, behind_y) = ways(i)
        first, rest = y_sum[i]
        if i in DIRECT_SUM:
            send(pb.at[i, yo], r1.at[i], y_sum_out, rest, {Y: yo})
            send(pb.at[i, ahead_y], r2.at[i], y_sum_out, rest, ahead)
        else:
            send(pb.at[i, yo], r1.at[i], y_sum_out, first, ahead)
        send(pb.at[i, behind_y], r3.at[i], y_sum_out, rest, behind)

    def stage1(i):
        if i in DIRECT_SUM:
            return
        (ahead, ahead_y), _ = ways(i)
        first, rest = y_sum[i]
        got(r1.at[i], first)
        pb[i, ahead_y] = (pb[i, ahead_y].astype(F32) + r1[i].astype(F32)).astype(BF)
        send(pb.at[i, ahead_y], r2.at[i], y_sum_out, rest, ahead)

    def stage2(i):
        total = pb[i, y].astype(F32)
        got(pb.at[0, pl.ds(0, 3 if i in DIRECT_SUM else 2)], y_sum[i][1])
        if i in DIRECT_SUM:
            total = total + r1[i].astype(F32)
        yb[i] = (total + r2[i].astype(F32) + r3[i].astype(F32)).astype(BF)
        for j in (2, 1, 3, 0):
            to = cross[j] if kinds[i] == 0 else along[j]
            if to is not None:
                rows = pl.ds(pl.multiple_of(((h + j) % 4) * HT, HT), HT)
                send(yb.at[i, rows, :], zr.at[i, j], z_sum_out, z_sum[i], to)

    def piece_of(i, first, count):
        half = 1 - l if kinds[i] == 0 else l
        return ob.at[slabs[i], half, pl.ds(pl.multiple_of(first, HT), count), :]

    def z_piece(i, which):
        return piece_of(i, y * QT + which * HT, HT)

    def quarter(i, which):
        return piece_of(i, which * QT, QT)

    def stage3(i):
        if kinds[i] == 0:
            got(zr.at[i], z_sum[i])
            total = zr[i, 0].astype(F32)
        else:
            got(zr.at[i, pl.ds(1, 3)], z_sum[i])
            total = yb[i, pl.ds(pl.multiple_of(h * HT, HT), HT), :].astype(F32)
        for j in range(1, 4):
            total = total + zr[i, j].astype(F32)
        piece = z_piece(i, h)
        piece[...] = total.astype(BF)
        first, rest = z_all[i]
        if i in DIRECT_SPREAD:
            first = rest
            send(piece, piece, z_all_out, rest, along[2])
        turn = (first, rest) if i % 2 == 0 else (rest, first)
        send(piece, piece, z_all_out, turn[0], along[1])
        send(piece, piece, z_all_out, turn[1], along[3])

    def stage4(i):
        if i in DIRECT_SPREAD:
            return
        behind, to = (hm, along[1]) if i % 2 == 0 else (hp, along[3])
        first, rest = z_all[i]
        piece = z_piece(i, behind)
        got(piece, first)
        send(piece, piece, z_all_out, rest, to)

    def stage5(i):
        got(zr.at[0, pl.ds(0, 3 if i in DIRECT_SPREAD else 2)], z_all[i][1])
        (ahead, _), (behind, _) = ways(i)
        first, rest = y_all[i]
        send(quarter(i, y), quarter(i, y), y_all_out, first, ahead)
        send(quarter(i, y), quarter(i, y), y_all_out, rest, behind)

    def stage6(i):
        (ahead, _), (_, behind_y) = ways(i)
        first, rest = y_all[i]
        got(quarter(i, behind_y), first)
        send(quarter(i, behind_y), quarter(i, behind_y), y_all_out, rest, ahead)

    def stage7(i):
        got(pb.at[0, pl.ds(0, 2)], y_all[i][1])

    steps = (
        lambda: outs.open(g_hbm, outer),
        lambda: (loads[0].wait(), down.open()),
        pre_open,
        lambda: acts_send(0, outer),
        own_gate_up,
        lambda: factors(l, mine),
        down.forward,
        gate_up.open,
        down.near,
        their_factors,
        down.far,
        own_product,
        lambda: quarter_product(0),
        near_products,
        gate_up.forward,
        far_product,
        gate_up.near,
        gate_up.far,
        their_grads,
        my_grads,
        grad_down.start,
        grad_down.relay,
        grad_down.finish,
        grad_gate.start,
        grad_gate.relay,
        grad_gate.finish,
        grad_down.multiply,
        lambda k: (acts_got() if k == 0 else None, grad_gate.multiply(k)),
        outs.spread,
        outs.forward,
    )
    stages = (stage0, stage1, stage2, stage3, stage4, stage5, stage6, stage7)
    assert (outlets.n, sems.n) == (OUTLETS, INLETS), (outlets.n, sems.n)
    for code in ORDER:
        with jax.named_scope(f"{code}"):
            if code >= 100:
                stages[code // 10 - 10](code % 10)
            elif code >= 40:
                steps[code // 10 + 22](code % 10)
            else:
                steps[code]()

    with jax.named_scope("sends"):
        for part in (down, gate_up, grad_down, grad_gate):
            part.drain()
        gone(gb.at[pl.ds(0, TOK), :], outs.outlet)
        gone(ab.at[pl.ds(0, TOK), :], acts_out)
        gone(gpt, pre_out)
        gone(ghs, product_out)
        gone(pb.at[pl.ds(0, 6)], y_sum_out)
        gone(pb.at[pl.ds(0, 6)], y_all_out)
        gone(zr.at[pl.ds(0, 7)], z_sum_out)
        gone(zr.at[pl.ds(0, 6)], z_all_out)


def finish(ob, wg, wd, gi_hbm, wg_hbm, wd_hbm, sem):
    copies = [pltpu.make_async_copy(wg, wg_hbm, sem.at[8]), pltpu.make_async_copy(wd, wd_hbm, sem.at[9])]
    for k in range(8):
        cols = pl.ds((k % 2) * DH + (k // 2) * SLAB, SLAB)
        copies.append(pltpu.make_async_copy(ob.at[k // 2, k % 2], gi_hbm.at[:, cols], sem.at[k]))
    for made in copies:
        made.start()
    for made in copies:
        made.wait()


def per_device(activations, grad_out, gate_pre, up_pre, gate_up, down_weight):
    hbm = pl.BlockSpec(memory_space=pl.ANY)
    vmem = pl.BlockSpec(memory_space=pltpu.VMEM)
    scratch = [
        pltpu.VMEM((ROWS, 2, FD), BF),
        pltpu.VMEM((2 * TOK, DH), BF),
        pltpu.VMEM((2 * TOK, DH), BF),
        pltpu.VMEM((DH, FD), BF),
        pltpu.VMEM((DH, FG), BF),
        pltpu.VMEM((2, FD, TOK), BF),
        pltpu.VMEM((2, FD, TOK), BF),
        pltpu.VMEM((2 * TOK, FD), F32),
        pltpu.VMEM((2 * TOK, FD), BF),
        pltpu.VMEM((2 * TOK, FD), BF),
        pltpu.VMEM((2 * TOK, FD), F32),
        pltpu.VMEM((2 * TOK, FD), F32),
        pltpu.VMEM((2 * TOK, FD), BF),
        pltpu.VMEM((2 * TOK, FG), BF),
        pltpu.VMEM((4, SLAB, FD), BF),
        pltpu.VMEM((4, ROWS, FD), BF),
        pltpu.VMEM((4, SLAB, FG), BF),
        pltpu.VMEM((4, ROWS, FG), BF),
        pltpu.VMEM((3, ROWS, FD), BF),
        pltpu.VMEM((3, ROWS, FG), BF),
        pltpu.VMEM((2, HALF, FD), BF),
        pltpu.VMEM((2, HALF, FG), BF),
        pltpu.VMEM((2, ROWS, FD), BF),
        pltpu.VMEM((2, ROWS, FG), BF),
        pltpu.VMEM((8, 4, QT, SLAB), BF),
        pltpu.VMEM((8, QT, SLAB), BF),
        pltpu.VMEM((8, QT, SLAB), BF),
        pltpu.VMEM((8, QT, SLAB), BF),
        pltpu.VMEM((8, QT, SLAB), BF),
        pltpu.VMEM((8, 4, HT, SLAB), BF),
        pltpu.SemaphoreType.DMA((6,)),
        pltpu.SemaphoreType.DMA((OUTLETS,)),
        pltpu.SemaphoreType.DMA((INLETS,)),
    ]
    held = pl.pallas_call(
        kernel,
        out_shape=(
            pltpu.VMEM((4, 2, TOK, SLAB), BF),
            pltpu.VMEM((ROWS, 2, FD), F32),
            pltpu.VMEM((ROWS, FD), F32),
        ),
        in_specs=[hbm] * 6,
        out_specs=(vmem, vmem, vmem),
        scratch_shapes=scratch,
        compiler_params=pltpu.CompilerParams(
            collective_id=0, has_side_effects=True, vmem_limit_bytes=56 * 1024 * 1024
        ),
        name="step",
    )(activations, grad_out, gate_pre.T, up_pre.T, gate_up, down_weight)
    held = [pltpu.with_memory_space_constraint(v, pltpu.VMEM) for v in held]
    return pl.pallas_call(
        finish,
        out_shape=(
            jax.ShapeDtypeStruct((TOK, D), BF),
            jax.ShapeDtypeStruct((ROWS, 2, FD), F32),
            jax.ShapeDtypeStruct((ROWS, FD), F32),
        ),
        in_specs=[vmem] * 3,
        out_specs=(hbm, hbm, hbm),
        scratch_shapes=[pltpu.SemaphoreType.DMA((10,))],
        compiler_params=pltpu.CompilerParams(vmem_limit_bytes=4 * 1024 * 1024),
        name="finish",
    )(*held)


def solution(mesh):
    split = Mesh(mesh.devices.reshape(2, 4, 2, 4, 4), (Z, X, C, H, Y))
    return jax.shard_map(
        per_device,
        mesh=split,
        in_specs=(
            P(DP, None),
            P(DP, None),
            P(DP, TENSOR),
            P(DP, TENSOR),
            P(DP, None, TENSOR),
            P(DP, TENSOR),
        ),
        out_specs=(P(DP, None), P(DP, None, TENSOR), P(DP, TENSOR)),
        check_vma=False,
    )
```

time: 92.6 us -> 87.3 us (0.943)
  Pallas kernels: 91.8 us -> 86.6 us
    pallas_call x1, Pallas kernels: 89.6 us -> 84.4 us  [per_device(): pl.pallas_call(kernel, out_shape=(pltpu.VMEM((4, 2, TOK, SLAB), BF), pltp...]
where the time goes in v4:
time: 87.3 us; the launch traced here: 87.2 us
  Pallas kernels  86.6 us (99%)
    pallas_call x1, Pallas kernels, per_device(): pl.pallas_call(kernel, out_shape=(pltpu.VMEM((4, 2, TOK, SLAB), BF), pltp...  84.4 us
    pallas_call x1, Pallas kernels, per_device(): pl.pallas_call(finish, out_shape=(jax.ShapeDtypeStruct((TOK, D), BF), jax...  2.21 us

profile of v4, /device:TPU:8, one launch (start us, length us, event | category | flops | bytes accessed | tf_op | source)
XLA Modules:
  0.0 87.2 jit_solution(13318754029893296772)
XLA Ops:
  0.6 84.4 %step.1 = (bf16[4,2,256,640]{3,2,1,0:T(8,128)(2,1)S(1)}, f32[320,2,448]{2,1,0:T(2,128)S(1)}, f32[320,448]{1,0:T(8,128)S(1)}) custom-call(bf16[256,5120]{1,0:T(8,128)(2,1)} %a_hbm.1, bf16[256,5120]{1,0:T(8,128)(2,1)} %g_hbm.1, bf16[448,256]{1,0:T(8,128)(2,1)} %bitcast.2, bf16[448,256]{1,0:T(8,128)(2,1)} %bitcast.3, bf16[320,2,448]{2,1,0:T(2,128)(2,1)} %gu_hbm.1, ...), custom_call_target="tpu_custom_call" | custom-call | tf_op jit(solution)/shard_map/step/pallas_call | solution.py:607
  85.0 2.2 %finish.1 = (bf16[256,5120]{1,0:T(8,128)(2,1)}, f32[320,2,448]{2,1,0:T(2,128)}, f32[320,448]{1,0:T(8,128)}) custom-call(bf16[4,2,256,640]{3,2,1,0:T(8,128)(2,1)S(1)} %get-tuple-element.6.ob, f32[320,2,448]{2,1,0:T(2,128)S(1)} %get-tuple-element.7.wg, f32[320,448]{1,0:T(8,128)S(1)} %get-tuple-element.8.wd), custom_call_target="tpu_custom_call" | custom-call | tf_op jit(solution)/shard_map/finish/pallas_call | solution.py:623

commit v5 on v4

--- a/solution.py
+++ b/solution.py
@@ -33,6 +33,21 @@
     124, 23, 116, 151, 132, 125, 117, 150, 133, 142, 134, 126, 143, 127, 161, 152, 144, 160, 135, 24, 136, 153,
     154, 137, 171, 155, 53, 156, 162, 164, 170, 157, 163, 25, 165, 166, 167, 173, 174, 175, 172, 177, 176,
 )
+
+
+def pack(ref, first, value):
+    n = value.shape[0]
+    value = value.astype(BF)
+    for tile in range(3):
+        ref[pl.ds(first + tile * n, n), :] = value[:, tile * 128 : (tile + 1) * 128]
+    tail = value[:, 384:]
+    ref[pl.ds(first + 3 * n, n // 2), :] = jnp.concatenate([tail[: n // 2], tail[n // 2 :]], axis=1)
+
+
+def unpack(ref, first, n):
+    tiles = [ref[pl.ds(first + tile * n, n), :] for tile in range(3)]
+    tail = ref[pl.ds(first + 3 * n, n // 2), :]
+    return jnp.concatenate(tiles + [jnp.concatenate([tail[:, :64], tail[:, 64:]], axis=0)], axis=1)
 
 
 class Sems:
@@ -63,6 +78,8 @@
     wg_out,
     wd_out,
     gu3,
+    dnb,
+    wp,
     gb,
     ab,
     wd,
@@ -146,7 +163,7 @@
 
     own_rows = slab_rows(x, c)
     loads = [
-        pltpu.make_async_copy(dn_hbm, wd.at[own_rows, :], lsem.at[0]),
+        pltpu.make_async_copy(dn_hbm, dnb, lsem.at[0]),
         pltpu.make_async_copy(gp_hbm, gpt.at[l], lsem.at[1]),
         pltpu.make_async_copy(up_hbm, upt.at[l], lsem.at[2]),
         pltpu.make_async_copy(gu_hbm, gu3, lsem.at[3]),
@@ -155,6 +172,10 @@
     ]
     for load in loads:
         load.start()
+    loads[0].wait()
+    for part in range(2):
+        pack(wp.at[4 * x + 2 * c + part], 0, dnb[pl.ds(part * HALF, HALF), :])
+    wd[own_rows, :] = dnb[...]
     pl.semaphore_wait(barrier, len(greeted))
 
     class Weights:
@@ -164,35 +185,60 @@
             self.first, self.second, self.last = sems.block(), sems.block(), sems.block()
             self.side = [sems.block() for _ in range(4)]
 
-        def put(self, rows, sem, to):
-            send(self.ref.at[rows, :], self.ref.at[rows, :], self.outlet, sem, to)
+        def block(self, xs, core, part=None):
+            return self.ref.at[slab_rows(xs, core, part), :]
+
+        def like(self, halves):
+            return self.ref.at[pl.ds(0, halves * HALF), :]
+
+        def ready(self, xs, core):
+            pass
+
+        def put(self, block, sem, to):
+            send(block, block, self.outlet, sem, to)
 
         def open(self):
-            self.put(slab_rows(x, c, 0), self.first, to_xp)
-            self.put(slab_rows(x, c, 1), self.first, to_xm)
-            self.put(slab_rows(x, c, 1), self.second, to_xp)
-            self.put(slab_rows(x, c, 0), self.second, to_xm)
-            self.put(own_rows, self.side[0], sib)
+            self.put(self.block(x, c, 0), self.first, to_xp)
+            self.put(self.block(x, c, 1), self.first, to_xm)
+            self.put(self.block(x, c, 1), self.second, to_xp)
+            self.put(self.block(x, c, 0), self.second, to_xm)
+            self.put(self.block(x, c), self.side[0], sib)
 
         def forward(self):
-            got(self.ref.at[pl.ds(0, ROWS), :], self.first)
-            self.put(slab_rows(xm, c, 0), self.last, to_xp)
-            self.put(slab_rows(xp, c, 1), self.last, to_xm)
+            got(self.like(2), self.first)
+            self.put(self.block(xm, c, 0), self.last, to_xp)
+            self.put(self.block(xp, c, 1), self.last, to_xm)
 
         def near(self):
-            got(self.ref.at[pl.ds(0, ROWS), :], self.second)
-            self.put(slab_rows(xm, c), self.side[1], sib)
-            self.put(slab_rows(xp, c), self.side[2], sib)
+            got(self.like(2), self.second)
+            self.put(self.block(xm, c), self.side[1], sib)
+            self.put(self.block(xp, c), self.side[2], sib)
+            self.ready(xm, c)
+            self.ready(xp, c)
 
         def far(self):
-            got(self.ref.at[pl.ds(0, ROWS), :], self.last)
-            self.put(slab_rows(xo, c), self.side[3], sib)
+            got(self.like(2), self.last)
+            self.put(self.block(xo, c), self.side[3], sib)
+            self.ready(xo, c)
 
         def side_got(self, k):
-            got(self.ref.at[pl.ds(0, ROWS), :], self.side[k])
+            got(self.like(2), self.side[k])
+            self.ready((x, xm, xp, xo)[k], 1 - c)
 
         def drain(self):
-            gone(self.ref.at[pl.ds(0, 7 * ROWS), :], self.outlet)
+            gone(self.like(14), self.outlet)
+
+    class Packed(Weights):
+        def block(self, xs, core, part=None):
+            first = 4 * xs + 2 * core
+            return wp.at[pl.ds(first, 2)] if part is None else wp.at[first + part]
+
+        def like(self, halves):
+            return wp.at[pl.ds(0, halves)]
+
+        def ready(self, xs, core):
+            for part in range(2):
+                self.ref[slab_rows(xs, core, part), :] = unpack(self.block(xs, core, part), 0, HALF)
 
     class Tokens:
         def __init__(self, ref):
@@ -237,7 +283,7 @@
         def far_got(self):
             got(self.ref.at[pl.ds(0, QT), :], self.far)
 
-    down, gate_up = Weights(wd), Weights(wg)
+    down, gate_up = Packed(wd), Weights(wg)
     outs = Tokens(gb)
     acts_sem, pre_sem, own_sem, quarter_sem = (sems.block() for _ in range(4))
     acts_out, pre_out, product_out = (outlets.block() for _ in range(3))
@@ -279,10 +325,16 @@
         got(gpt, pre_sem)
         factors(1 - l, theirs)
 
-    def product(rows, part, sem):
+    def packed_at(group, quarter, count):
+        return pl.multiple_of(group * (TOK * 7 // 2) + quarter * (QT * 7 // 2), 32), count * 7 // 2
+
+    def product(group, quarter, count, part, sem):
+        rows = pl.ds(pl.multiple_of(group * TOK + quarter * QT, QT), count)
         ghf[rows, :] = part
-        ghs[rows, :] = part.astype(BF)
-        send(ghs.at[rows, :], ghr.at[rows, :], product_out, sem, inner)
+        first, size = packed_at(group, quarter, count)
+        pack(ghs, first, part)
+        block = pl.ds(first, size)
+        send(ghs.at[block, :], ghr.at[block, :], product_out, sem, inner)
 
     def slab_product(xs):
         where = pl.ds(pl.multiple_of(xs * SLAB, 128), SLAB)
@@ -294,14 +346,14 @@
             down.side_got(k)
         part = slab_product(x) + slab_product(xm) + slab_product(xp)
         down.side_got(3)
-        product(mine, part + slab_product(xo), own_sem)
+        product(l, 0, TOK, part + slab_product(xo), own_sem)
 
     def quarter_rows(group, k):
         return pl.ds(pl.multiple_of(group * TOK + quarters[k] * QT, QT), QT)
 
     def quarter_product(k):
         rows = quarter_rows(1 - l, k)
-        product(rows, jnp.dot(gb[rows, :], wd[...], preferred_element_type=F32), quarter_sem)
+        product(1 - l, quarters[k], QT, jnp.dot(gb[rows, :], wd[...], preferred_element_type=F32), quarter_sem)
 
     def near_products():
         outs.near_got()
@@ -377,18 +429,20 @@
     grad_down = Grad(gb, hid, dws_d, dwr_d, vs_d, r1_d, r2_d, wd_out)
     grad_gate = Grad(ab, ghb, dws_g, dwr_g, vs_g, r1_g, r2_g, wg_out)
 
-    def hidden_grads(rows):
-        total = ghf[rows, :] + ghr[rows, :].astype(F32)
+    def hidden_grads(group, quarter, count):
+        rows = pl.ds(pl.multiple_of(group * TOK + quarter * QT, QT), count)
+        total = ghf[rows, :] + unpack(ghr, packed_at(group, quarter, count)[0], count).astype(F32)
         ghb[rows, pl.ds(0, FD)] = (total * dgate_s[rows, :]).astype(BF)
         ghb[rows, pl.ds(FD, FD)] = (total * silu_s[rows, :]).astype(BF)
 
     def their_grads():
-        got(ghr.at[theirs, :], own_sem)
-        hidden_grads(theirs)
+        got(ghr.at[pl.ds(0, TOK * 7 // 2), :], own_sem)
+        hidden_grads(1 - l, 0, TOK)
 
     def my_grads():
-        got(ghr.at[mine, :], quarter_sem)
-        hidden_grads(mine)
+        got(ghr.at[pl.ds(0, TOK * 7 // 2), :], quarter_sem)
+        for k in range(4):
+            hidden_grads(l, k, QT)
 
     slabs = [(x, xm, xp, xo)[k] for k, _ in CHUNKS]
     kinds = [kind for _, kind in CHUNKS]
@@ -501,7 +555,7 @@
 
     steps = (
         lambda: outs.open(g_hbm, outer),
-        lambda: (loads[0].wait(), down.open()),
+        down.open,
         pre_open,
         lambda: acts_send(0, outer),
         own_gate_up,
@@ -571,6 +625,8 @@
     vmem = pl.BlockSpec(memory_space=pltpu.VMEM)
     scratch = [
         pltpu.VMEM((ROWS, 2, FD), BF),
+        pltpu.VMEM((ROWS, FD), BF),
+        pltpu.VMEM((16, HALF * 7 // 2, 128), BF),
         pltpu.VMEM((2 * TOK, DH), BF),
         pltpu.VMEM((2 * TOK, DH), BF),
         pltpu.VMEM((DH, FD), BF),
@@ -578,8 +634,8 @@
         pltpu.VMEM((2, FD, TOK), BF),
         pltpu.VMEM((2, FD, TOK), BF),
         pltpu.VMEM((2 * TOK, FD), F32),
-        pltpu.VMEM((2 * TOK, FD), BF),
-        pltpu.VMEM((2 * TOK, FD), BF),
+        pltpu.VMEM((TOK * 7, 128), BF),
+        pltpu.VMEM((TOK * 7, 128), BF),
         pltpu.VMEM((2 * TOK, FD), F32),
         pltpu.VMEM((2 * TOK, FD), F32),
         pltpu.VMEM((2 * TOK, FD), BF),

time: 87.3 us -> 86.7 us (level)
  Pallas kernels: 86.6 us -> 85.5 us
    pallas_call x1, Pallas kernels: 84.4 us -> 83.2 us  [per_device(): pl.pallas_call(kernel, out_shape=(pltpu.VMEM((4, 2, TOK, SLAB), BF), pltp...]
where the time goes in v5:
time: 86.7 us; the launch traced here: 86.1 us
  Pallas kernels  85.5 us (99%)
    pallas_call x1, Pallas kernels, per_device(): pl.pallas_call(kernel, out_shape=(pltpu.VMEM((4, 2, TOK, SLAB), BF), pltp...  83.2 us
    pallas_call x1, Pallas kernels, per_device(): pl.pallas_call(finish, out_shape=(jax.ShapeDtypeStruct((TOK, D), BF), jax...  2.21 us

profile of v5, /device:TPU:8, one launch (start us, length us, event | category | flops | bytes accessed | tf_op | source)
XLA Modules:
  0.0 86.1 jit_solution(16858729391845849399)
XLA Ops:
  0.6 83.2 %step.1 = (bf16[4,2,256,640]{3,2,1,0:T(8,128)(2,1)S(1)}, f32[320,2,448]{2,1,0:T(2,128)S(1)}, f32[320,448]{1,0:T(8,128)S(1)}) custom-call(bf16[256,5120]{1,0:T(8,128)(2,1)} %a_hbm.1, bf16[256,5120]{1,0:T(8,128)(2,1)} %g_hbm.1, bf16[448,256]{1,0:T(8,128)(2,1)} %bitcast.2, bf16[448,256]{1,0:T(8,128)(2,1)} %bitcast.3, bf16[320,2,448]{2,1,0:T(2,128)(2,1)} %gu_hbm.1, ...), custom_call_target="tpu_custom_call" | custom-call | tf_op jit(solution)/shard_map/step/pallas_call | solution.py:663
  83.9 2.2 %finish.1 = (bf16[256,5120]{1,0:T(8,128)(2,1)}, f32[320,2,448]{2,1,0:T(2,128)}, f32[320,448]{1,0:T(8,128)}) custom-call(bf16[4,2,256,640]{3,2,1,0:T(8,128)(2,1)S(1)} %get-tuple-element.6.ob, f32[320,2,448]{2,1,0:T(2,128)S(1)} %get-tuple-element.7.wg, f32[320,448]{1,0:T(8,128)S(1)} %get-tuple-element.8.wd), custom_call_target="tpu_custom_call" | custom-call | tf_op jit(solution)/shard_map/finish/pallas_call | solution.py:679

commit v6 on v5

--- a/solution.py
+++ b/solution.py
@@ -30,8 +30,8 @@
 ORDER = (
     1, 2, 0, 3, 6, 60, 4, 7, 8, 61, 10, 70, 5, 11, 71, 13, 14, 9, 12, 15, 18, 100, 16, 40, 41, 42, 101, 102, 19,
     43, 20, 17, 103, 104, 120, 50, 121, 51, 112, 105, 21, 130, 113, 114, 131, 106, 122, 115, 52, 123, 107, 22,
-    124, 23, 116, 151, 132, 125, 117, 150, 133, 142, 134, 126, 143, 127, 161, 152, 144, 160, 135, 24, 136, 153,
-    154, 137, 171, 155, 53, 156, 162, 164, 170, 157, 163, 25, 165, 166, 167, 173, 174, 175, 172, 177, 176,
+    124, 23, 116, 151, 132, 125, 117, 150, 133, 142, 134, 126, 143, 127, 161, 53, 152, 144, 160, 135, 24, 136,
+    153, 154, 137, 171, 155, 156, 162, 164, 170, 157, 163, 25, 165, 166, 167, 173, 174, 175, 172, 177, 176,
 )
 
 
@@ -610,10 +610,11 @@
 
 
 def finish(ob, wg, wd, gi_hbm, wg_hbm, wd_hbm, sem):
-    copies = [pltpu.make_async_copy(wg, wg_hbm, sem.at[8]), pltpu.make_async_copy(wd, wd_hbm, sem.at[9])]
+    copies = []
     for k in range(8):
         cols = pl.ds((k % 2) * DH + (k // 2) * SLAB, SLAB)
         copies.append(pltpu.make_async_copy(ob.at[k // 2, k % 2], gi_hbm.at[:, cols], sem.at[k]))
+    copies += [pltpu.make_async_copy(wg, wg_hbm, sem.at[8]), pltpu.make_async_copy(wd, wd_hbm, sem.at[9])]
     for made in copies:
         made.start()
     for made in copies:

time: 86.7 us -> 87 us (level)
  no operation moved by 1% of the time
where the time goes in v6:
time: 87 us; the launch traced here: 86.8 us
  Pallas kernels  86.1 us (99%)
    pallas_call x1, Pallas kernels, per_device(): pl.pallas_call(kernel, out_shape=(pltpu.VMEM((4, 2, TOK, SLAB), BF), pltp...  83.9 us
    pallas_call x1, Pallas kernels, per_device(): pl.pallas_call(finish, out_shape=(jax.ShapeDtypeStruct((TOK, D), BF), jax...  2.22 us

profile of v6, /device:TPU:8, one launch (start us, length us, event | category | flops | bytes accessed | tf_op | source)
XLA Modules:
  0.0 86.8 jit_solution(18348793256282113511)
XLA Ops:
  0.6 83.9 %step.1 = (bf16[4,2,256,640]{3,2,1,0:T(8,128)(2,1)S(1)}, f32[320,2,448]{2,1,0:T(2,128)S(1)}, f32[320,448]{1,0:T(8,128)S(1)}) custom-call(bf16[256,5120]{1,0:T(8,128)(2,1)} %a_hbm.1, bf16[256,5120]{1,0:T(8,128)(2,1)} %g_hbm.1, bf16[448,256]{1,0:T(8,128)(2,1)} %bitcast.2, bf16[448,256]{1,0:T(8,128)(2,1)} %bitcast.3, bf16[320,2,448]{2,1,0:T(2,128)(2,1)} %gu_hbm.1, ...), custom_call_target="tpu_custom_call" | custom-call | tf_op jit(solution)/shard_map/step/pallas_call | solution.py:664
  84.5 2.2 %finish.1 = (bf16[256,5120]{1,0:T(8,128)(2,1)}, f32[320,2,448]{2,1,0:T(2,128)}, f32[320,448]{1,0:T(8,128)}) custom-call(bf16[4,2,256,640]{3,2,1,0:T(8,128)(2,1)S(1)} %get-tuple-element.6.ob, f32[320,2,448]{2,1,0:T(2,128)S(1)} %get-tuple-element.7.wg, f32[320,448]{1,0:T(8,128)S(1)} %get-tuple-element.8.wd), custom_call_target="tpu_custom_call" | custom-call | tf_op jit(solution)/shard_map/finish/pallas_call | solution.py:680
